TPU v7x, 32 devices: a 4x4x1 block of a 4x4x8 slice. The times are simulated.
32 devices in a mesh: dp: 1 (over z), ctx: 32 (over y, x, core).
Axes of the slice: x: 4, y: 4, z: 1, core: 2. Of those that a mesh axis runs over, the one named last changes fastest.
The devices are a block of a 4x4x8 slice.
Arguments:
- q_seq: bfloat16 [1, 8192, 16, 128], P('dp', 'ctx')
- k_seq: bfloat16 [1, 8192, 4, 128], P('dp', 'ctx')
- v_seq: bfloat16 [1, 8192, 4, 128], P('dp', 'ctx')
- do_seq: bfloat16 [1, 8192, 16, 128], P('dp', 'ctx')
Outputs:
- output 1: bfloat16 [1, 8192, 16, 128], P('dp', 'ctx')
- output 2: bfloat16 [1, 8192, 16, 128], P('dp', 'ctx')
- output 3: bfloat16 [1, 8192, 4, 128], P('dp', 'ctx')
- output 4: bfloat16 [1, 8192, 4, 128], P('dp', 'ctx')
All inputs are finite; a program needn't handle non-finite values.
Results may differ from a plain program's by a relative error of at most 0.00873153.
Values are sent between devices in bfloat16 or wider.
A program may use at most 768 MiB of HBM per device.

v0:
```python
import jax
import jax.numpy as jnp
from jax import lax
from jax.sharding import PartitionSpec as P

WINDOW = 4096
NEG_BIG = -1e30


def fwd_update(state, q_five, k_blk, v_blk, keep_mask, sm_scale):
    m_run, l_run, o_acc = state
    scores = jnp.einsum('bqhgd,bkhd->bhgqk', q_five, k_blk, preferred_element_type=jnp.float32) * sm_scale
    scores = jnp.where(keep_mask, scores, NEG_BIG)
    m_new = jnp.maximum(m_run, jnp.max(scores, axis=-1))
    rescale = jnp.exp(m_run - m_new)
    p_blk = jnp.exp(scores - m_new[..., None])
    l_new = rescale * l_run + jnp.sum(p_blk, axis=-1)
    pv_blk = jnp.einsum('bhgqk,bkhd->bhgqd', p_blk.astype(jnp.bfloat16), v_blk, preferred_element_type=jnp.float32)
    return m_new, l_new, rescale[..., None] * o_acc + pv_blk


def bwd_block(q_five, do_five, log_sum, d_row, k_blk, v_blk, keep_mask, sm_scale):
    scores = jnp.einsum('bqhgd,bkhd->bhgqk', q_five, k_blk, preferred_element_type=jnp.float32) * sm_scale
    p_blk = jnp.exp(jnp.where(keep_mask, scores, NEG_BIG) - log_sum[..., None])
    d_prob = jnp.einsum('bqhgd,bkhd->bhgqk', do_five, v_blk, preferred_element_type=jnp.float32)
    d_score = (p_blk * (d_prob - d_row[..., None])).astype(jnp.bfloat16)
    dv_part = jnp.einsum('bhgqk,bqhgd->bkhd', p_blk.astype(jnp.bfloat16), do_five, preferred_element_type=jnp.float32)
    dq_part = jnp.einsum('bhgqk,bkhd->bqhgd', d_score, k_blk, preferred_element_type=jnp.float32) * sm_scale
    dk_part = jnp.einsum('bhgqk,bqhgd->bkhd', d_score, q_five, preferred_element_type=jnp.float32) * sm_scale
    return dq_part, dk_part, dv_part


def solution(mesh):
    n_ctx = mesh.shape['ctx']
    seq_spec = P('dp', 'ctx', None, None)
    shift_perm = [(j, (j + 1) % n_ctx) for j in range(n_ctx)]

    def local_attn(q_loc, k_loc, v_loc, do_loc):
        n_batch, chunk_len, q_heads, head_dim = q_loc.shape
        kv_heads = k_loc.shape[2]
        q_group = q_heads // kv_heads
        n_blocks = WINDOW // chunk_len
        sm_scale = head_dim ** -0.5
        dev_idx = lax.axis_index('ctx')
        five_shape = (n_batch, chunk_len, kv_heads, q_group, head_dim)
        q_five = q_loc.reshape(five_shape)
        do_five = do_loc.reshape(five_shape)
        offsets = jnp.arange(chunk_len)[:, None] - jnp.arange(chunk_len)[None, :]

        def block_mask(step_id):
            dist = step_id * chunk_len + offsets
            return (dist >= 0) & (dist < WINDOW) & (dev_idx >= step_id)

        stat_shape = (n_batch, kv_heads, q_group, chunk_len)
        init = (jnp.full(stat_shape, NEG_BIG, jnp.float32), jnp.zeros(stat_shape, jnp.float32), jnp.zeros(stat_shape + (head_dim,), jnp.float32))
        state = fwd_update(init, q_five, k_loc, v_loc, block_mask(0), sm_scale)

        def fwd_body(step_id, carry):
            kv_blk, run_state = carry
            kv_blk = lax.ppermute(kv_blk, 'ctx', shift_perm)
            run_state = fwd_update(run_state, q_five, kv_blk[0], kv_blk[1], block_mask(step_id), sm_scale)
            return kv_blk, run_state

        _, (m_run, l_run, o_acc) = lax.fori_loop(1, n_blocks + 1, fwd_body, ((k_loc, v_loc), state))
        log_sum = m_run + jnp.log(l_run)
        o_five = jnp.transpose((o_acc / l_run[..., None]).astype(jnp.bfloat16), (0, 3, 1, 2, 4))
        d_row = jnp.einsum('bqhgd,bqhgd->bhgq', do_five, o_five, preferred_element_type=jnp.float32)
        dq_acc, dk_acc, dv_acc = bwd_block(q_five, do_five, log_sum, d_row, k_loc, v_loc, block_mask(0), sm_scale)

        def bwd_body(step_id, carry):
            travel, dq_run = carry
            k_blk, v_blk, dk_run, dv_run = lax.ppermute(travel, 'ctx', shift_perm)
            dq_part, dk_part, dv_part = bwd_block(q_five, do_five, log_sum, d_row, k_blk, v_blk, block_mask(step_id), sm_scale)
            return (k_blk, v_blk, dk_run + dk_part, dv_run + dv_part), dq_run + dq_part

        (_, _, dk_acc, dv_acc), dq_acc = lax.fori_loop(1, n_blocks + 1, bwd_body, ((k_loc, v_loc, dk_acc, dv_acc), dq_acc))
        home_perm = [(j, (j - n_blocks) % n_ctx) for j in range(n_ctx)]
        dk_home, dv_home = lax.ppermute((dk_acc, dv_acc), 'ctx', home_perm)
        return (o_five.reshape(q_loc.shape), dq_acc.astype(jnp.bfloat16).reshape(q_loc.shape), dk_home.astype(jnp.bfloat16), dv_home.astype(jnp.bfloat16))

    return jax.shard_map(local_attn, mesh=mesh, in_specs=(seq_spec, seq_spec, seq_spec, seq_spec), out_specs=(seq_spec, seq_spec, seq_spec, seq_spec), check_vma=False)
```

profile of v0, /device:TPU:96, one launch (start us, length us, event | category | flops | bytes accessed | tf_op | source)
XLA Modules:
  0.0 716.0 jit_solution(12953245670098255501)
XLA Ops:
  9.4 258.2 %while.44 = (s32[]{:T(128)}, bf16[1,256,4,128]{3,1,2,0:T(8,128)(2,1)}, bf16[1,256,4,128]{3,1,2,0:T(8,128)(2,1)}, f32[1,4,4,256]{3,2,1,0:T(4,128)S(1)}, f32[1,4,4...) while((s32[]{:T(128)}, ...), condition=%wide.region_5.6_spmd.clone, body=%wide.region_2.5_spmd.clone.sunk | while | flops 549859328 | bytes 22020304 | solution.py:64
  10.9 9.0 %collective-permute-done = bf16[1,256,4,128]{3,1,2,0:T(8,128)(2,1)} collective-permute-done((bf16[1,256,4,128]{3,1,2,0:T(8,128)(2,1)}, bf16[1,256,4,128]{3,1,2,0:T(8,128)(2,1)}, u32[]{:S(2)}, u32[]{:S(2)}) %collective-permute-start) | collective-permute-done | bytes 262176 | tf_op jit(solution)/shard_map/while/body/eval_jaxpr/ppermute | solution.py:60
  27.1 8.9 %collective-permute-done = bf16[1,256,4,128]{3,1,2,0:T(8,128)(2,1)} collective-permute-done((bf16[1,256,4,128]{3,1,2,0:T(8,128)(2,1)}, bf16[1,256,4,128]{3,1,2,0:T(8,128)(2,1)}, u32[]{:S(2)}, u32[]{:S(2)}) %collective-permute-start) | collective-permute-done | bytes 262176 | tf_op jit(solution)/shard_map/while/body/eval_jaxpr/ppermute | solution.py:60
  43.2 8.9 %collective-permute-done = bf16[1,256,4,128]{3,1,2,0:T(8,128)(2,1)} collective-permute-done((bf16[1,256,4,128]{3,1,2,0:T(8,128)(2,1)}, bf16[1,256,4,128]{3,1,2,0:T(8,128)(2,1)}, u32[]{:S(2)}, u32[]{:S(2)}) %collective-permute-start) | collective-permute-done | bytes 262176 | tf_op jit(solution)/shard_map/while/body/eval_jaxpr/ppermute | solution.py:60
  59.2 8.9 %collective-permute-done = bf16[1,256,4,128]{3,1,2,0:T(8,128)(2,1)} collective-permute-done((bf16[1,256,4,128]{3,1,2,0:T(8,128)(2,1)}, bf16[1,256,4,128]{3,1,2,0:T(8,128)(2,1)}, u32[]{:S(2)}, u32[]{:S(2)}) %collective-permute-start) | collective-permute-done | bytes 262176 | tf_op jit(solution)/shard_map/while/body/eval_jaxpr/ppermute | solution.py:60
  75.3 8.9 %collective-permute-done = bf16[1,256,4,128]{3,1,2,0:T(8,128)(2,1)} collective-permute-done((bf16[1,256,4,128]{3,1,2,0:T(8,128)(2,1)}, bf16[1,256,4,128]{3,1,2,0:T(8,128)(2,1)}, u32[]{:S(2)}, u32[]{:S(2)}) %collective-permute-start) | collective-permute-done | bytes 262176 | tf_op jit(solution)/shard_map/while/body/eval_jaxpr/ppermute | solution.py:60
  91.3 8.9 %collective-permute-done = bf16[1,256,4,128]{3,1,2,0:T(8,128)(2,1)} collective-permute-done((bf16[1,256,4,128]{3,1,2,0:T(8,128)(2,1)}, bf16[1,256,4,128]{3,1,2,0:T(8,128)(2,1)}, u32[]{:S(2)}, u32[]{:S(2)}) %collective-permute-start) | collective-permute-done | bytes 262176 | tf_op jit(solution)/shard_map/while/body/eval_jaxpr/ppermute | solution.py:60
  107.4 8.9 %collective-permute-done = bf16[1,256,4,128]{3,1,2,0:T(8,128)(2,1)} collective-permute-done((bf16[1,256,4,128]{3,1,2,0:T(8,128)(2,1)}, bf16[1,256,4,128]{3,1,2,0:T(8,128)(2,1)}, u32[]{:S(2)}, u32[]{:S(2)}) %collective-permute-start) | collective-permute-done | bytes 262176 | tf_op jit(solution)/shard_map/while/body/eval_jaxpr/ppermute | solution.py:60
  123.4 8.9 %collective-permute-done = bf16[1,256,4,128]{3,1,2,0:T(8,128)(2,1)} collective-permute-done((bf16[1,256,4,128]{3,1,2,0:T(8,128)(2,1)}, bf16[1,256,4,128]{3,1,2,0:T(8,128)(2,1)}, u32[]{:S(2)}, u32[]{:S(2)}) %collective-permute-start) | collective-permute-done | bytes 262176 | tf_op jit(solution)/shard_map/while/body/eval_jaxpr/ppermute | solution.py:60
  139.5 8.9 %collective-permute-done = bf16[1,256,4,128]{3,1,2,0:T(8,128)(2,1)} collective-permute-done((bf16[1,256,4,128]{3,1,2,0:T(8,128)(2,1)}, bf16[1,256,4,128]{3,1,2,0:T(8,128)(2,1)}, u32[]{:S(2)}, u32[]{:S(2)}) %collective-permute-start) | collective-permute-done | bytes 262176 | tf_op jit(solution)/shard_map/while/body/eval_jaxpr/ppermute | solution.py:60
  155.5 8.9 %collective-permute-done = bf16[1,256,4,128]{3,1,2,0:T(8,128)(2,1)} collective-permute-done((bf16[1,256,4,128]{3,1,2,0:T(8,128)(2,1)}, bf16[1,256,4,128]{3,1,2,0:T(8,128)(2,1)}, u32[]{:S(2)}, u32[]{:S(2)}) %collective-permute-start) | collective-permute-done | bytes 262176 | tf_op jit(solution)/shard_map/while/body/eval_jaxpr/ppermute | solution.py:60
  171.6 8.9 %collective-permute-done = bf16[1,256,4,128]{3,1,2,0:T(8,128)(2,1)} collective-permute-done((bf16[1,256,4,128]{3,1,2,0:T(8,128)(2,1)}, bf16[1,256,4,128]{3,1,2,0:T(8,128)(2,1)}, u32[]{:S(2)}, u32[]{:S(2)}) %collective-permute-start) | collective-permute-done | bytes 262176 | tf_op jit(solution)/shard_map/while/body/eval_jaxpr/ppermute | solution.py:60
  187.7 8.9 %collective-permute-done = bf16[1,256,4,128]{3,1,2,0:T(8,128)(2,1)} collective-permute-done((bf16[1,256,4,128]{3,1,2,0:T(8,128)(2,1)}, bf16[1,256,4,128]{3,1,2,0:T(8,128)(2,1)}, u32[]{:S(2)}, u32[]{:S(2)}) %collective-permute-start) | collective-permute-done | bytes 262176 | tf_op jit(solution)/shard_map/while/body/eval_jaxpr/ppermute | solution.py:60
  203.7 8.9 %collective-permute-done = bf16[1,256,4,128]{3,1,2,0:T(8,128)(2,1)} collective-permute-done((bf16[1,256,4,128]{3,1,2,0:T(8,128)(2,1)}, bf16[1,256,4,128]{3,1,2,0:T(8,128)(2,1)}, u32[]{:S(2)}, u32[]{:S(2)}) %collective-permute-start) | collective-permute-done | bytes 262176 | tf_op jit(solution)/shard_map/while/body/eval_jaxpr/ppermute | solution.py:60
  219.8 8.9 %collective-permute-done = bf16[1,256,4,128]{3,1,2,0:T(8,128)(2,1)} collective-permute-done((bf16[1,256,4,128]{3,1,2,0:T(8,128)(2,1)}, bf16[1,256,4,128]{3,1,2,0:T(8,128)(2,1)}, u32[]{:S(2)}, u32[]{:S(2)}) %collective-permute-start) | collective-permute-done | bytes 262176 | tf_op jit(solution)/shard_map/while/body/eval_jaxpr/ppermute | solution.py:60
  235.8 8.9 %collective-permute-done = bf16[1,256,4,128]{3,1,2,0:T(8,128)(2,1)} collective-permute-done((bf16[1,256,4,128]{3,1,2,0:T(8,128)(2,1)}, bf16[1,256,4,128]{3,1,2,0:T(8,128)(2,1)}, u32[]{:S(2)}, u32[]{:S(2)}) %collective-permute-start) | collective-permute-done | bytes 262176 | tf_op jit(solution)/shard_map/while/body/eval_jaxpr/ppermute | solution.py:60
  251.9 8.9 %collective-permute-done = bf16[1,256,4,128]{3,1,2,0:T(8,128)(2,1)} collective-permute-done((bf16[1,256,4,128]{3,1,2,0:T(8,128)(2,1)}, bf16[1,256,4,128]{3,1,2,0:T(8,128)(2,1)}, u32[]{:S(2)}, u32[]{:S(2)}) %collective-permute-start) | collective-permute-done | bytes 262176 | tf_op jit(solution)/shard_map/while/body/eval_jaxpr/ppermute | solution.py:60
  281.0 421.4 %while.45 = (s32[]{:T(128)}, bf16[1,256,4,128]{3,1,2,0:T(8,128)(2,1)}, bf16[1,256,4,128]{3,1,2,0:T(8,128)(2,1)}, f32[1,256,4,128]{3,1,2,0:T(8,128)}, f32[1,256,4...) while((s32[]{:T(128)}, ...), condition=%wide.region_7.8_spmd.clone, body=%wide.region_6.7_spmd.clone.sunk | while | flops 1354498048 | bytes 41926992 | solution.py:76
  281.3 8.9 %collective-permute-done.2 = bf16[1,256,4,128]{3,1,2,0:T(8,128)(2,1)S(1)} collective-permute-done((bf16[1,256,4,128]{3,1,2,0:T(8,128)(2,1)}, bf16[1,256,4,128]{3,1,2,0:T(8,128)(2,1)S(1)}, u32[]{:S(2)}, u32[]{:S(2)}) %collective-permute-start.2) | collective-permute-done | bytes 262176 | tf_op jit(solution)/shard_map/while/body/eval_jaxpr/ppermute | solution.py:72
  307.5 8.9 %collective-permute-done.2 = bf16[1,256,4,128]{3,1,2,0:T(8,128)(2,1)S(1)} collective-permute-done((bf16[1,256,4,128]{3,1,2,0:T(8,128)(2,1)}, bf16[1,256,4,128]{3,1,2,0:T(8,128)(2,1)S(1)}, u32[]{:S(2)}, u32[]{:S(2)}) %collective-permute-start.2) | collective-permute-done | bytes 262176 | tf_op jit(solution)/shard_map/while/body/eval_jaxpr/ppermute | solution.py:72
  333.7 8.9 %collective-permute-done.2 = bf16[1,256,4,128]{3,1,2,0:T(8,128)(2,1)S(1)} collective-permute-done((bf16[1,256,4,128]{3,1,2,0:T(8,128)(2,1)}, bf16[1,256,4,128]{3,1,2,0:T(8,128)(2,1)S(1)}, u32[]{:S(2)}, u32[]{:S(2)}) %collective-permute-start.2) | collective-permute-done | bytes 262176 | tf_op jit(solution)/shard_map/while/body/eval_jaxpr/ppermute | solution.py:72
  359.9 8.9 %collective-permute-done.2 = bf16[1,256,4,128]{3,1,2,0:T(8,128)(2,1)S(1)} collective-permute-done((bf16[1,256,4,128]{3,1,2,0:T(8,128)(2,1)}, bf16[1,256,4,128]{3,1,2,0:T(8,128)(2,1)S(1)}, u32[]{:S(2)}, u32[]{:S(2)}) %collective-permute-start.2) | collective-permute-done | bytes 262176 | tf_op jit(solution)/shard_map/while/body/eval_jaxpr/ppermute | solution.py:72
  386.1 8.9 %collective-permute-done.2 = bf16[1,256,4,128]{3,1,2,0:T(8,128)(2,1)S(1)} collective-permute-done((bf16[1,256,4,128]{3,1,2,0:T(8,128)(2,1)}, bf16[1,256,4,128]{3,1,2,0:T(8,128)(2,1)S(1)}, u32[]{:S(2)}, u32[]{:S(2)}) %collective-permute-start.2) | collective-permute-done | bytes 262176 | tf_op jit(solution)/shard_map/while/body/eval_jaxpr/ppermute | solution.py:72
  412.3 8.9 %collective-permute-done.2 = bf16[1,256,4,128]{3,1,2,0:T(8,128)(2,1)S(1)} collective-permute-done((bf16[1,256,4,128]{3,1,2,0:T(8,128)(2,1)}, bf16[1,256,4,128]{3,1,2,0:T(8,128)(2,1)S(1)}, u32[]{:S(2)}, u32[]{:S(2)}) %collective-permute-start.2) | collective-permute-done | bytes 262176 | tf_op jit(solution)/shard_map/while/body/eval_jaxpr/ppermute | solution.py:72
  438.5 8.9 %collective-permute-done.2 = bf16[1,256,4,128]{3,1,2,0:T(8,128)(2,1)S(1)} collective-permute-done((bf16[1,256,4,128]{3,1,2,0:T(8,128)(2,1)}, bf16[1,256,4,128]{3,1,2,0:T(8,128)(2,1)S(1)}, u32[]{:S(2)}, u32[]{:S(2)}) %collective-permute-start.2) | collective-permute-done | bytes 262176 | tf_op jit(solution)/shard_map/while/body/eval_jaxpr/ppermute | solution.py:72
  464.7 8.9 %collective-permute-done.2 = bf16[1,256,4,128]{3,1,2,0:T(8,128)(2,1)S(1)} collective-permute-done((bf16[1,256,4,128]{3,1,2,0:T(8,128)(2,1)}, bf16[1,256,4,128]{3,1,2,0:T(8,128)(2,1)S(1)}, u32[]{:S(2)}, u32[]{:S(2)}) %collective-permute-start.2) | collective-permute-done | bytes 262176 | tf_op jit(solution)/shard_map/while/body/eval_jaxpr/ppermute | solution.py:72
  490.9 8.9 %collective-permute-done.2 = bf16[1,256,4,128]{3,1,2,0:T(8,128)(2,1)S(1)} collective-permute-done((bf16[1,256,4,128]{3,1,2,0:T(8,128)(2,1)}, bf16[1,256,4,128]{3,1,2,0:T(8,128)(2,1)S(1)}, u32[]{:S(2)}, u32[]{:S(2)}) %collective-permute-start.2) | collective-permute-done | bytes 262176 | tf_op jit(solution)/shard_map/while/body/eval_jaxpr/ppermute | solution.py:72
  517.1 8.9 %collective-permute-done.2 = bf16[1,256,4,128]{3,1,2,0:T(8,128)(2,1)S(1)} collective-permute-done((bf16[1,256,4,128]{3,1,2,0:T(8,128)(2,1)}, bf16[1,256,4,128]{3,1,2,0:T(8,128)(2,1)S(1)}, u32[]{:S(2)}, u32[]{:S(2)}) %collective-permute-start.2) | collective-permute-done | bytes 262176 | tf_op jit(solution)/shard_map/while/body/eval_jaxpr/ppermute | solution.py:72
  543.3 8.9 %collective-permute-done.2 = bf16[1,256,4,128]{3,1,2,0:T(8,128)(2,1)S(1)} collective-permute-done((bf16[1,256,4,128]{3,1,2,0:T(8,128)(2,1)}, bf16[1,256,4,128]{3,1,2,0:T(8,128)(2,1)S(1)}, u32[]{:S(2)}, u32[]{:S(2)}) %collective-permute-start.2) | collective-permute-done | bytes 262176 | tf_op jit(solution)/shard_map/while/body/eval_jaxpr/ppermute | solution.py:72
  569.5 8.9 %collective-permute-done.2 = bf16[1,256,4,128]{3,1,2,0:T(8,128)(2,1)S(1)} collective-permute-done((bf16[1,256,4,128]{3,1,2,0:T(8,128)(2,1)}, bf16[1,256,4,128]{3,1,2,0:T(8,128)(2,1)S(1)}, u32[]{:S(2)}, u32[]{:S(2)}) %collective-permute-start.2) | collective-permute-done | bytes 262176 | tf_op jit(solution)/shard_map/while/body/eval_jaxpr/ppermute | solution.py:72
  595.7 8.9 %collective-permute-done.2 = bf16[1,256,4,128]{3,1,2,0:T(8,128)(2,1)S(1)} collective-permute-done((bf16[1,256,4,128]{3,1,2,0:T(8,128)(2,1)}, bf16[1,256,4,128]{3,1,2,0:T(8,128)(2,1)S(1)}, u32[]{:S(2)}, u32[]{:S(2)}) %collective-permute-start.2) | collective-permute-done | bytes 262176 | tf_op jit(solution)/shard_map/while/body/eval_jaxpr/ppermute | solution.py:72
  621.9 8.9 %collective-permute-done.2 = bf16[1,256,4,128]{3,1,2,0:T(8,128)(2,1)S(1)} collective-permute-done((bf16[1,256,4,128]{3,1,2,0:T(8,128)(2,1)}, bf16[1,256,4,128]{3,1,2,0:T(8,128)(2,1)S(1)}, u32[]{:S(2)}, u32[]{:S(2)}) %collective-permute-start.2) | collective-permute-done | bytes 262176 | tf_op jit(solution)/shard_map/while/body/eval_jaxpr/ppermute | solution.py:72
  (523 shorter events, 446.7 us)
Async XLA Ops:
  281.0 18.4 %collective-permute-start.4 = (f32[1,256,4,128]{3,1,2,0:T(8,128)}, f32[1,256,4,128]{3,1,2,0:T(8,128)}, u32[]{:S(2)}, u32[]{:S(2)}) collective-permute-start(f32[1,256,4,128]{3,1,2,0:T(8,128)} %get-tuple-element.647), channel_id=1, source_target_pairs={{0,1},{1,2},{2,3},{3,4},{4,5},{5,6},{6,7},{7,8},{8,9},{9,10},{10,1... | collective-permute-start | bytes 1572872 | tf_op jit(solution)/shard_map/while/body/eval_jaxpr/ppermute | solution.py:72
  281.0 23.1 %collective-permute-start.5 = (f32[1,256,4,128]{3,1,2,0:T(8,128)}, f32[1,256,4,128]{3,1,2,0:T(8,128)}, u32[]{:S(2)}, u32[]{:S(2)}) collective-permute-start(f32[1,256,4,128]{3,1,2,0:T(8,128)} %get-tuple-element.648), channel_id=1, source_target_pairs={{0,1},{1,2},{2,3},{3,4},{4,5},{5,6},{6,7},{7,8},{8,9},{9,10},{10,1... | collective-permute-start | bytes 1572872 | tf_op jit(solution)/shard_map/while/body/eval_jaxpr/ppermute | solution.py:72
  307.2 18.4 %collective-permute-start.4 = (f32[1,256,4,128]{3,1,2,0:T(8,128)}, f32[1,256,4,128]{3,1,2,0:T(8,128)}, u32[]{:S(2)}, u32[]{:S(2)}) collective-permute-start(f32[1,256,4,128]{3,1,2,0:T(8,128)} %get-tuple-element.647), channel_id=1, source_target_pairs={{0,1},{1,2},{2,3},{3,4},{4,5},{5,6},{6,7},{7,8},{8,9},{9,10},{10,1... | collective-permute-start | bytes 1572872 | tf_op jit(solution)/shard_map/while/body/eval_jaxpr/ppermute | solution.py:72
  307.2 23.1 %collective-permute-start.5 = (f32[1,256,4,128]{3,1,2,0:T(8,128)}, f32[1,256,4,128]{3,1,2,0:T(8,128)}, u32[]{:S(2)}, u32[]{:S(2)}) collective-permute-start(f32[1,256,4,128]{3,1,2,0:T(8,128)} %get-tuple-element.648), channel_id=1, source_target_pairs={{0,1},{1,2},{2,3},{3,4},{4,5},{5,6},{6,7},{7,8},{8,9},{9,10},{10,1... | collective-permute-start | bytes 1572872 | tf_op jit(solution)/shard_map/while/body/eval_jaxpr/ppermute | solution.py:72
  333.4 18.4 %collective-permute-start.4 = (f32[1,256,4,128]{3,1,2,0:T(8,128)}, f32[1,256,4,128]{3,1,2,0:T(8,128)}, u32[]{:S(2)}, u32[]{:S(2)}) collective-permute-start(f32[1,256,4,128]{3,1,2,0:T(8,128)} %get-tuple-element.647), channel_id=1, source_target_pairs={{0,1},{1,2},{2,3},{3,4},{4,5},{5,6},{6,7},{7,8},{8,9},{9,10},{10,1... | collective-permute-start | bytes 1572872 | tf_op jit(solution)/shard_map/while/body/eval_jaxpr/ppermute | solution.py:72
  333.4 23.1 %collective-permute-start.5 = (f32[1,256,4,128]{3,1,2,0:T(8,128)}, f32[1,256,4,128]{3,1,2,0:T(8,128)}, u32[]{:S(2)}, u32[]{:S(2)}) collective-permute-start(f32[1,256,4,128]{3,1,2,0:T(8,128)} %get-tuple-element.648), channel_id=1, source_target_pairs={{0,1},{1,2},{2,3},{3,4},{4,5},{5,6},{6,7},{7,8},{8,9},{9,10},{10,1... | collective-permute-start | bytes 1572872 | tf_op jit(solution)/shard_map/while/body/eval_jaxpr/ppermute | solution.py:72
  359.6 18.4 %collective-permute-start.4 = (f32[1,256,4,128]{3,1,2,0:T(8,128)}, f32[1,256,4,128]{3,1,2,0:T(8,128)}, u32[]{:S(2)}, u32[]{:S(2)}) collective-permute-start(f32[1,256,4,128]{3,1,2,0:T(8,128)} %get-tuple-element.647), channel_id=1, source_target_pairs={{0,1},{1,2},{2,3},{3,4},{4,5},{5,6},{6,7},{7,8},{8,9},{9,10},{10,1... | collective-permute-start | bytes 1572872 | tf_op jit(solution)/shard_map/while/body/eval_jaxpr/ppermute | solution.py:72
  359.6 23.1 %collective-permute-start.5 = (f32[1,256,4,128]{3,1,2,0:T(8,128)}, f32[1,256,4,128]{3,1,2,0:T(8,128)}, u32[]{:S(2)}, u32[]{:S(2)}) collective-permute-start(f32[1,256,4,128]{3,1,2,0:T(8,128)} %get-tuple-element.648), channel_id=1, source_target_pairs={{0,1},{1,2},{2,3},{3,4},{4,5},{5,6},{6,7},{7,8},{8,9},{9,10},{10,1... | collective-permute-start | bytes 1572872 | tf_op jit(solution)/shard_map/while/body/eval_jaxpr/ppermute | solution.py:72
  385.8 18.4 %collective-permute-start.4 = (f32[1,256,4,128]{3,1,2,0:T(8,128)}, f32[1,256,4,128]{3,1,2,0:T(8,128)}, u32[]{:S(2)}, u32[]{:S(2)}) collective-permute-start(f32[1,256,4,128]{3,1,2,0:T(8,128)} %get-tuple-element.647), channel_id=1, source_target_pairs={{0,1},{1,2},{2,3},{3,4},{4,5},{5,6},{6,7},{7,8},{8,9},{9,10},{10,1... | collective-permute-start | bytes 1572872 | tf_op jit(solution)/shard_map/while/body/eval_jaxpr/ppermute | solution.py:72
  385.9 23.1 %collective-permute-start.5 = (f32[1,256,4,128]{3,1,2,0:T(8,128)}, f32[1,256,4,128]{3,1,2,0:T(8,128)}, u32[]{:S(2)}, u32[]{:S(2)}) collective-permute-start(f32[1,256,4,128]{3,1,2,0:T(8,128)} %get-tuple-element.648), channel_id=1, source_target_pairs={{0,1},{1,2},{2,3},{3,4},{4,5},{5,6},{6,7},{7,8},{8,9},{9,10},{10,1... | collective-permute-start | bytes 1572872 | tf_op jit(solution)/shard_map/while/body/eval_jaxpr/ppermute | solution.py:72
  412.0 18.4 %collective-permute-start.4 = (f32[1,256,4,128]{3,1,2,0:T(8,128)}, f32[1,256,4,128]{3,1,2,0:T(8,128)}, u32[]{:S(2)}, u32[]{:S(2)}) collective-permute-start(f32[1,256,4,128]{3,1,2,0:T(8,128)} %get-tuple-element.647), channel_id=1, source_target_pairs={{0,1},{1,2},{2,3},{3,4},{4,5},{5,6},{6,7},{7,8},{8,9},{9,10},{10,1... | collective-permute-start | bytes 1572872 | tf_op jit(solution)/shard_map/while/body/eval_jaxpr/ppermute | solution.py:72
  412.1 23.1 %collective-permute-start.5 = (f32[1,256,4,128]{3,1,2,0:T(8,128)}, f32[1,256,4,128]{3,1,2,0:T(8,128)}, u32[]{:S(2)}, u32[]{:S(2)}) collective-permute-start(f32[1,256,4,128]{3,1,2,0:T(8,128)} %get-tuple-element.648), channel_id=1, source_target_pairs={{0,1},{1,2},{2,3},{3,4},{4,5},{5,6},{6,7},{7,8},{8,9},{9,10},{10,1... | collective-permute-start | bytes 1572872 | tf_op jit(solution)/shard_map/while/body/eval_jaxpr/ppermute | solution.py:72
  438.2 18.4 %collective-permute-start.4 = (f32[1,256,4,128]{3,1,2,0:T(8,128)}, f32[1,256,4,128]{3,1,2,0:T(8,128)}, u32[]{:S(2)}, u32[]{:S(2)}) collective-permute-start(f32[1,256,4,128]{3,1,2,0:T(8,128)} %get-tuple-element.647), channel_id=1, source_target_pairs={{0,1},{1,2},{2,3},{3,4},{4,5},{5,6},{6,7},{7,8},{8,9},{9,10},{10,1... | collective-permute-start | bytes 1572872 | tf_op jit(solution)/shard_map/while/body/eval_jaxpr/ppermute | solution.py:72
  438.3 23.1 %collective-permute-start.5 = (f32[1,256,4,128]{3,1,2,0:T(8,128)}, f32[1,256,4,128]{3,1,2,0:T(8,128)}, u32[]{:S(2)}, u32[]{:S(2)}) collective-permute-start(f32[1,256,4,128]{3,1,2,0:T(8,128)} %get-tuple-element.648), channel_id=1, source_target_pairs={{0,1},{1,2},{2,3},{3,4},{4,5},{5,6},{6,7},{7,8},{8,9},{9,10},{10,1... | collective-permute-start | bytes 1572872 | tf_op jit(solution)/shard_map/while/body/eval_jaxpr/ppermute | solution.py:72
  464.5 18.4 %collective-permute-start.4 = (f32[1,256,4,128]{3,1,2,0:T(8,128)}, f32[1,256,4,128]{3,1,2,0:T(8,128)}, u32[]{:S(2)}, u32[]{:S(2)}) collective-permute-start(f32[1,256,4,128]{3,1,2,0:T(8,128)} %get-tuple-element.647), channel_id=1, source_target_pairs={{0,1},{1,2},{2,3},{3,4},{4,5},{5,6},{6,7},{7,8},{8,9},{9,10},{10,1... | collective-permute-start | bytes 1572872 | tf_op jit(solution)/shard_map/while/body/eval_jaxpr/ppermute | solution.py:72
  464.5 23.1 %collective-permute-start.5 = (f32[1,256,4,128]{3,1,2,0:T(8,128)}, f32[1,256,4,128]{3,1,2,0:T(8,128)}, u32[]{:S(2)}, u32[]{:S(2)}) collective-permute-start(f32[1,256,4,128]{3,1,2,0:T(8,128)} %get-tuple-element.648), channel_id=1, source_target_pairs={{0,1},{1,2},{2,3},{3,4},{4,5},{5,6},{6,7},{7,8},{8,9},{9,10},{10,1... | collective-permute-start | bytes 1572872 | tf_op jit(solution)/shard_map/while/body/eval_jaxpr/ppermute | solution.py:72
  490.7 18.4 %collective-permute-start.4 = (f32[1,256,4,128]{3,1,2,0:T(8,128)}, f32[1,256,4,128]{3,1,2,0:T(8,128)}, u32[]{:S(2)}, u32[]{:S(2)}) collective-permute-start(f32[1,256,4,128]{3,1,2,0:T(8,128)} %get-tuple-element.647), channel_id=1, source_target_pairs={{0,1},{1,2},{2,3},{3,4},{4,5},{5,6},{6,7},{7,8},{8,9},{9,10},{10,1... | collective-permute-start | bytes 1572872 | tf_op jit(solution)/shard_map/while/body/eval_jaxpr/ppermute | solution.py:72
  490.7 23.1 %collective-permute-start.5 = (f32[1,256,4,128]{3,1,2,0:T(8,128)}, f32[1,256,4,128]{3,1,2,0:T(8,128)}, u32[]{:S(2)}, u32[]{:S(2)}) collective-permute-start(f32[1,256,4,128]{3,1,2,0:T(8,128)} %get-tuple-element.648), channel_id=1, source_target_pairs={{0,1},{1,2},{2,3},{3,4},{4,5},{5,6},{6,7},{7,8},{8,9},{9,10},{10,1... | collective-permute-start | bytes 1572872 | tf_op jit(solution)/shard_map/while/body/eval_jaxpr/ppermute | solution.py:72
  516.9 18.4 %collective-permute-start.4 = (f32[1,256,4,128]{3,1,2,0:T(8,128)}, f32[1,256,4,128]{3,1,2,0:T(8,128)}, u32[]{:S(2)}, u32[]{:S(2)}) collective-permute-start(f32[1,256,4,128]{3,1,2,0:T(8,128)} %get-tuple-element.647), channel_id=1, source_target_pairs={{0,1},{1,2},{2,3},{3,4},{4,5},{5,6},{6,7},{7,8},{8,9},{9,10},{10,1... | collective-permute-start | bytes 1572872 | tf_op jit(solution)/shard_map/while/body/eval_jaxpr/ppermute | solution.py:72
  516.9 23.1 %collective-permute-start.5 = (f32[1,256,4,128]{3,1,2,0:T(8,128)}, f32[1,256,4,128]{3,1,2,0:T(8,128)}, u32[]{:S(2)}, u32[]{:S(2)}) collective-permute-start(f32[1,256,4,128]{3,1,2,0:T(8,128)} %get-tuple-element.648), channel_id=1, source_target_pairs={{0,1},{1,2},{2,3},{3,4},{4,5},{5,6},{6,7},{7,8},{8,9},{9,10},{10,1... | collective-permute-start | bytes 1572872 | tf_op jit(solution)/shard_map/while/body/eval_jaxpr/ppermute | solution.py:72
  543.1 18.4 %collective-permute-start.4 = (f32[1,256,4,128]{3,1,2,0:T(8,128)}, f32[1,256,4,128]{3,1,2,0:T(8,128)}, u32[]{:S(2)}, u32[]{:S(2)}) collective-permute-start(f32[1,256,4,128]{3,1,2,0:T(8,128)} %get-tuple-element.647), channel_id=1, source_target_pairs={{0,1},{1,2},{2,3},{3,4},{4,5},{5,6},{6,7},{7,8},{8,9},{9,10},{10,1... | collective-permute-start | bytes 1572872 | tf_op jit(solution)/shard_map/while/body/eval_jaxpr/ppermute | solution.py:72
  543.1 23.1 %collective-permute-start.5 = (f32[1,256,4,128]{3,1,2,0:T(8,128)}, f32[1,256,4,128]{3,1,2,0:T(8,128)}, u32[]{:S(2)}, u32[]{:S(2)}) collective-permute-start(f32[1,256,4,128]{3,1,2,0:T(8,128)} %get-tuple-element.648), channel_id=1, source_target_pairs={{0,1},{1,2},{2,3},{3,4},{4,5},{5,6},{6,7},{7,8},{8,9},{9,10},{10,1... | collective-permute-start | bytes 1572872 | tf_op jit(solution)/shard_map/while/body/eval_jaxpr/ppermute | solution.py:72
  569.3 18.4 %collective-permute-start.4 = (f32[1,256,4,128]{3,1,2,0:T(8,128)}, f32[1,256,4,128]{3,1,2,0:T(8,128)}, u32[]{:S(2)}, u32[]{:S(2)}) collective-permute-start(f32[1,256,4,128]{3,1,2,0:T(8,128)} %get-tuple-element.647), channel_id=1, source_target_pairs={{0,1},{1,2},{2,3},{3,4},{4,5},{5,6},{6,7},{7,8},{8,9},{9,10},{10,1... | collective-permute-start | bytes 1572872 | tf_op jit(solution)/shard_map/while/body/eval_jaxpr/ppermute | solution.py:72
  569.3 23.1 %collective-permute-start.5 = (f32[1,256,4,128]{3,1,2,0:T(8,128)}, f32[1,256,4,128]{3,1,2,0:T(8,128)}, u32[]{:S(2)}, u32[]{:S(2)}) collective-permute-start(f32[1,256,4,128]{3,1,2,0:T(8,128)} %get-tuple-element.648), channel_id=1, source_target_pairs={{0,1},{1,2},{2,3},{3,4},{4,5},{5,6},{6,7},{7,8},{8,9},{9,10},{10,1... | collective-permute-start | bytes 1572872 | tf_op jit(solution)/shard_map/while/body/eval_jaxpr/ppermute | solution.py:72
  595.5 18.4 %collective-permute-start.4 = (f32[1,256,4,128]{3,1,2,0:T(8,128)}, f32[1,256,4,128]{3,1,2,0:T(8,128)}, u32[]{:S(2)}, u32[]{:S(2)}) collective-permute-start(f32[1,256,4,128]{3,1,2,0:T(8,128)} %get-tuple-element.647), channel_id=1, source_target_pairs={{0,1},{1,2},{2,3},{3,4},{4,5},{5,6},{6,7},{7,8},{8,9},{9,10},{10,1... | collective-permute-start | bytes 1572872 | tf_op jit(solution)/shard_map/while/body/eval_jaxpr/ppermute | solution.py:72
  595.5 23.1 %collective-permute-start.5 = (f32[1,256,4,128]{3,1,2,0:T(8,128)}, f32[1,256,4,128]{3,1,2,0:T(8,128)}, u32[]{:S(2)}, u32[]{:S(2)}) collective-permute-start(f32[1,256,4,128]{3,1,2,0:T(8,128)} %get-tuple-element.648), channel_id=1, source_target_pairs={{0,1},{1,2},{2,3},{3,4},{4,5},{5,6},{6,7},{7,8},{8,9},{9,10},{10,1... | collective-permute-start | bytes 1572872 | tf_op jit(solution)/shard_map/while/body/eval_jaxpr/ppermute | solution.py:72
  621.7 18.4 %collective-permute-start.4 = (f32[1,256,4,128]{3,1,2,0:T(8,128)}, f32[1,256,4,128]{3,1,2,0:T(8,128)}, u32[]{:S(2)}, u32[]{:S(2)}) collective-permute-start(f32[1,256,4,128]{3,1,2,0:T(8,128)} %get-tuple-element.647), channel_id=1, source_target_pairs={{0,1},{1,2},{2,3},{3,4},{4,5},{5,6},{6,7},{7,8},{8,9},{9,10},{10,1... | collective-permute-start | bytes 1572872 | tf_op jit(solution)/shard_map/while/body/eval_jaxpr/ppermute | solution.py:72
  621.7 23.1 %collective-permute-start.5 = (f32[1,256,4,128]{3,1,2,0:T(8,128)}, f32[1,256,4,128]{3,1,2,0:T(8,128)}, u32[]{:S(2)}, u32[]{:S(2)}) collective-permute-start(f32[1,256,4,128]{3,1,2,0:T(8,128)} %get-tuple-element.648), channel_id=1, source_target_pairs={{0,1},{1,2},{2,3},{3,4},{4,5},{5,6},{6,7},{7,8},{8,9},{9,10},{10,1... | collective-permute-start | bytes 1572872 | tf_op jit(solution)/shard_map/while/body/eval_jaxpr/ppermute | solution.py:72
  647.9 18.4 %collective-permute-start.4 = (f32[1,256,4,128]{3,1,2,0:T(8,128)}, f32[1,256,4,128]{3,1,2,0:T(8,128)}, u32[]{:S(2)}, u32[]{:S(2)}) collective-permute-start(f32[1,256,4,128]{3,1,2,0:T(8,128)} %get-tuple-element.647), channel_id=1, source_target_pairs={{0,1},{1,2},{2,3},{3,4},{4,5},{5,6},{6,7},{7,8},{8,9},{9,10},{10,1... | collective-permute-start | bytes 1572872 | tf_op jit(solution)/shard_map/while/body/eval_jaxpr/ppermute | solution.py:72
  647.9 23.1 %collective-permute-start.5 = (f32[1,256,4,128]{3,1,2,0:T(8,128)}, f32[1,256,4,128]{3,1,2,0:T(8,128)}, u32[]{:S(2)}, u32[]{:S(2)}) collective-permute-start(f32[1,256,4,128]{3,1,2,0:T(8,128)} %get-tuple-element.648), channel_id=1, source_target_pairs={{0,1},{1,2},{2,3},{3,4},{4,5},{5,6},{6,7},{7,8},{8,9},{9,10},{10,1... | collective-permute-start | bytes 1572872 | tf_op jit(solution)/shard_map/while/body/eval_jaxpr/ppermute | solution.py:72
  674.1 18.4 %collective-permute-start.4 = (f32[1,256,4,128]{3,1,2,0:T(8,128)}, f32[1,256,4,128]{3,1,2,0:T(8,128)}, u32[]{:S(2)}, u32[]{:S(2)}) collective-permute-start(f32[1,256,4,128]{3,1,2,0:T(8,128)} %get-tuple-element.647), channel_id=1, source_target_pairs={{0,1},{1,2},{2,3},{3,4},{4,5},{5,6},{6,7},{7,8},{8,9},{9,10},{10,1... | collective-permute-start | bytes 1572872 | tf_op jit(solution)/shard_map/while/body/eval_jaxpr/ppermute | solution.py:72
  674.1 25.2 %collective-permute-start.5 = (f32[1,256,4,128]{3,1,2,0:T(8,128)}, f32[1,256,4,128]{3,1,2,0:T(8,128)}, u32[]{:S(2)}, u32[]{:S(2)}) collective-permute-start(f32[1,256,4,128]{3,1,2,0:T(8,128)} %get-tuple-element.648), channel_id=1, source_target_pairs={{0,1},{1,2},{2,3},{3,4},{4,5},{5,6},{6,7},{7,8},{8,9},{9,10},{10,1... | collective-permute-start | bytes 1572872 | tf_op jit(solution)/shard_map/while/body/eval_jaxpr/ppermute | solution.py:72
  (95 other events, 952.3 us)
where the time goes:
time: 720 us; the launch traced here: 716 us
  waiting for transfers between devices  354 us (49%)
  matrix products  234 us (32%)
  local copies, waits for them, and re-layouts  92 us (13%)
  other arithmetic  22.3 us (3%)
  starting transfers between devices  10.2 us (1%)
    ppermute x64, waiting for transfers between devices, bwd_body(): k_blk, v_blk, dk_run, dv_run = lax.ppermute(travel, 'ctx', shift_perm)  212 us
    ppermute x32, waiting for transfers between devices, fwd_body(): kv_blk = lax.ppermute(kv_blk, 'ctx', shift_perm)  142 us
    while x112, local copies, waits for them, and re-layouts  76.5 us
    dot_general x17, matrix products, bwd_block(): jnp.einsum('bhgqk,bqhgd->bkhd', p_blk.astype(jnp.bfloat16), do_five, pref...  53.1 us
    dot_general x17, matrix products, bwd_block(): jnp.einsum('bhgqk,bqhgd->bkhd', d_score, q_five, preferred_element_type=j...  43.2 us
    dot_general x17, matrix products, bwd_block(): jnp.einsum('bqhgd,bkhd->bhgqk', do_five, v_blk, preferred_element_type=jn...  38 us
    dot_general x17, matrix products, fwd_update(): jnp.einsum('bhgqk,bkhd->bhgqd', p_blk.astype(jnp.bfloat16), v_blk, prefer...  30.1 us
    dot_general x17, matrix products, bwd_block(): jnp.einsum('bhgqk,bkhd->bqhgd', d_score, k_blk, preferred_element_type=jn...  29.7 us
  transfers between devices with their start and end apart: 98, of which 65 were waited for; matrix products, arithmetic and copies ran while one was open for 33% of the time, Pallas kernels for 0%

commit v1 on v0

v1 whole, which is shorter than its diff:
```python
import functools

import jax
import jax.numpy as jnp
from jax import lax
from jax.experimental import pallas as pl
from jax.experimental.pallas import tpu as pltpu
from jax.sharding import PartitionSpec as P

WINDOW = 4096
NEG = -1e30
LOG2E = 1.4426950408889634
F32 = jnp.float32
BF16 = jnp.bfloat16


def dot(a, b):
    return jnp.dot(a, b, preferred_element_type=F32)


def fold8(x, op):
    n = x.shape[0] // 8
    acc = x[0:8]
    for t in range(1, n):
        acc = op(acc, x[8 * t:8 * t + 8])
    return acc


def attn_kernel(inner, n_win, sm_scale, q_ref, do_ref, k_ref, v_ref, o_ref, dq_ref, dk_ref, dv_ref,
                kt, vt, qt, dot_t, s_scr, acc_t, m_scr, l_scr, lse_scr, d_scr):
    n_q, group, chunk, dim = q_ref.shape
    n_kv = k_ref.shape[0]
    row_pos = lax.rem(lax.axis_index('ctx'), inner)
    c_exp = sm_scale * LOG2E

    def prep(j, _):
        kt[j] = k_ref[j].T
        vt[j] = v_ref[j].T
        dk_ref[j] = jnp.zeros((chunk, dim), F32)
        dv_ref[j] = jnp.zeros((chunk, dim), F32)
        return 0

    lax.fori_loop(0, n_kv, prep, 0)
    rows = lax.broadcasted_iota(jnp.int32, (chunk, chunk), 0)
    cols = lax.broadcasted_iota(jnp.int32, (chunk, chunk), 1)

    def cs(h):
        return slice(h * chunk, (h + 1) * chunk)

    def one_chunk(i, _):
        g = i * inner + row_pos
        lo = jnp.maximum(g - n_win, 0)
        n = g - lo + 1
        for h in range(group):
            qt[:, cs(h)] = q_ref[i, h].T
            dot_t[:, cs(h)] = do_ref[i, h].T
        m_scr[...] = jnp.full(m_scr.shape, NEG, F32)
        l_scr[...] = jnp.zeros(l_scr.shape, F32)

        def score(jj, keep):
            kb = k_ref[lo + jj]
            for h in range(group):
                s = dot(kb, qt[:, cs(h)])
                if keep is not None:
                    s = jnp.where(keep, s, NEG)
                s_scr[jj, :, cs(h)] = s
                m_scr[:, cs(h)] = jnp.maximum(m_scr[:, cs(h)], fold8(s, jnp.maximum))

        old_edge = g >= n_win
        first = jnp.where(old_edge, 1, 0)

        @pl.when(old_edge)
        def _():
            score(0, rows > cols)

        def score_body(jj, _):
            score(jj, None)
            return 0

        lax.fori_loop(first, n - 1, score_body, 0)
        score(n - 1, rows <= cols)
        m_row = jnp.max(m_scr[...], axis=0, keepdims=True) * c_exp
        m_scr[...] = jnp.broadcast_to(m_row, m_scr.shape)
        acc_t[...] = jnp.zeros(acc_t.shape, F32)

        def pv_body(jj, _):
            vb = vt[lo + jj]
            for h in range(group):
                p = jnp.exp2(s_scr[jj, :, cs(h)] * c_exp - m_scr[0:1, cs(h)])
                l_scr[:, cs(h)] += fold8(p, jnp.add)
                acc_t[:, cs(h)] += dot(vb, p.astype(BF16))
            return 0

        lax.fori_loop(0, n, pv_body, 0)
        l_row = jnp.sum(l_scr[...], axis=0, keepdims=True)
        lse_scr[...] = jnp.broadcast_to(m_scr[0:1] + jnp.log2(l_row), lse_scr.shape)
        for h in range(group):
            o_t = (acc_t[:, cs(h)] / l_row[:, cs(h)]).astype(BF16)
            d = jnp.sum(o_t.astype(F32) * dot_t[:, cs(h)].astype(F32), axis=0, keepdims=True)
            d_scr[:, cs(h)] = jnp.broadcast_to(d, (8, chunk))
            o_ref[i, h] = o_t.T
        acc_t[...] = jnp.zeros(acc_t.shape, F32)

        def bwd_body(jj, _):
            j = lo + jj
            vb = v_ref[j]
            kb = kt[j]
            dv = dv_ref[j]
            dk = dk_ref[j]
            for h in range(group):
                p = jnp.exp2(s_scr[jj, :, cs(h)] * c_exp - lse_scr[0:1, cs(h)])
                dp = dot(vb, dot_t[:, cs(h)])
                ds = (p * (dp - d_scr[0:1, cs(h)])).astype(BF16)
                dv = dv + dot(p.astype(BF16), do_ref[i, h])
                dk = dk + dot(ds, q_ref[i, h])
                acc_t[:, cs(h)] += dot(kb, ds)
            dv_ref[j] = dv
            dk_ref[j] = dk
            return 0

        lax.fori_loop(0, n, bwd_body, 0)
        for h in range(group):
            dq_ref[i, h] = (acc_t[:, cs(h)] * sm_scale).astype(BF16).T
        return 0

    lax.fori_loop(0, n_q, one_chunk, 0)


def solution(mesh):
    n_ctx = mesh.shape['ctx']
    seq_spec = P('dp', 'ctx', None, None)

    def local_attn(q_loc, k_loc, v_loc, do_loc):
        n_batch, chunk, q_heads, dim = q_loc.shape
        kv_heads = k_loc.shape[2]
        group = q_heads // kv_heads
        inner = n_ctx // kv_heads
        n_win = WINDOW // chunk
        n_q = kv_heads
        cols = [[y * inner + r for y in range(kv_heads)] for r in range(inner)]
        rows = [[y * inner + r for r in range(inner)] for y in range(kv_heads)]

        def split(x, per):
            x = jnp.transpose(x[0], (1, 0, 2)).reshape(kv_heads, per, chunk, dim)
            return lax.all_to_all(x, 'ctx', 0, 0, axis_index_groups=cols)

        def merge(x, per):
            x = lax.all_to_all(x, 'ctx', 0, 0, axis_index_groups=cols)
            return jnp.transpose(x.reshape(kv_heads * per, chunk, dim), (1, 0, 2))[None]

        q4, do4 = split(q_loc, group), split(do_loc, group)
        k4, v4 = split(k_loc, 1), split(v_loc, 1)
        k_all = lax.all_gather(k4[:, 0], 'ctx', axis_index_groups=rows, axis=1).reshape(n_ctx, chunk, dim)
        v_all = lax.all_gather(v4[:, 0], 'ctx', axis_index_groups=rows, axis=1).reshape(n_ctx, chunk, dim)
        wide = group * chunk
        vm = pl.BlockSpec(memory_space=pltpu.VMEM)
        o4, dq4, dk, dv = pl.pallas_call(
            functools.partial(attn_kernel, inner, n_win, dim ** -0.5),
            out_shape=(jax.ShapeDtypeStruct(q4.shape, BF16), jax.ShapeDtypeStruct(q4.shape, BF16),
                       jax.ShapeDtypeStruct(k_all.shape, F32), jax.ShapeDtypeStruct(k_all.shape, F32)),
            in_specs=[vm] * 4,
            out_specs=(vm,) * 4,
            scratch_shapes=[
                pltpu.VMEM((n_ctx, dim, chunk), BF16), pltpu.VMEM((n_ctx, dim, chunk), BF16),
                pltpu.VMEM((dim, wide), BF16), pltpu.VMEM((dim, wide), BF16),
                pltpu.VMEM((n_win + 1, chunk, wide), F32), pltpu.VMEM((dim, wide), F32),
                pltpu.VMEM((8, wide), F32), pltpu.VMEM((8, wide), F32),
                pltpu.VMEM((8, wide), F32), pltpu.VMEM((8, wide), F32),
            ],
            compiler_params=pltpu.CompilerParams(vmem_limit_bytes=60 * 1024 * 1024),
            name='attn_core',
        )(q4, do4, k_all, v_all)
        sm_scale = dim ** -0.5

        def reduce(x):
            x = lax.psum_scatter(x.reshape(n_q, inner, chunk, dim), 'ctx', scatter_dimension=1, axis_index_groups=rows)
            return x[:, None]

        dk4 = (reduce(dk) * sm_scale).astype(BF16)
        dv4 = reduce(dv).astype(BF16)
        return merge(o4, group), merge(dq4, group), merge(dk4, 1), merge(dv4, 1)

    return jax.shard_map(local_attn, mesh=mesh, in_specs=(seq_spec,) * 4, out_specs=(seq_spec,) * 4, check_vma=False)
```

time: 720 us -> 276 us (0.38)
  the two profiles are of different devices: /device:TPU:96 before, /device:TPU:97 now
where the time goes in v1:
time: 276 us; the launch traced here: 273 us
  Pallas kernels  87.7 us (32%)
  waiting for transfers between devices  82.4 us (30%)
  blocking collectives  37.6 us (14%)
  local copies, waits for them, and re-layouts  28.6 us (10%)
  starting transfers between devices  18.8 us (7%)
  between operations  13.9 us (5%)
  other arithmetic  3.58 us (1%)
    pallas_call x1, Pallas kernels, local_attn(): pl.pallas_call(functools.partial(attn_kernel, inner, n_win, dim ** (-0.5)...  87.7 us
    reduce_scatter x2, waiting for transfers between devices, reduce(): lax.psum_scatter(x.reshape(n_q, inner, chunk, dim), 'ctx', scatter_dimens...  56.2 us
    all_to_all x2, blocking collectives, split(): return lax.all_to_all(x, 'ctx', 0, 0, axis_index_groups=cols)  20.4 us
    all_to_all x1, blocking collectives, merge(): x = lax.all_to_all(x, 'ctx', 0, 0, axis_index_groups=cols)  17.3 us
    all_gather x1, waiting for transfers between devices, local_attn(): lax.all_gather(v4[:, 0], 'ctx', axis_index_groups=rows, axis=1)  14.7 us
    all_to_all x3, starting transfers between devices, merge(): x = lax.all_to_all(x, 'ctx', 0, 0, axis_index_groups=cols)  11.3 us
    all_to_all x2, waiting for transfers between devices, split(): return lax.all_to_all(x, 'ctx', 0, 0, axis_index_groups=cols)  10.2 us
    reshape x2, local copies, waits for them, and re-layouts, reduce(): x.reshape(n_q, inner, chunk, dim)  9.24 us
  transfers between devices with their start and end apart: 9, of which 5 were waited for; matrix products, arithmetic and copies ran while one was open for 9% of the time, Pallas kernels for 0%

profile of v1, /device:TPU:97, one launch (start us, length us, event | category | flops | bytes accessed | tf_op | source)
XLA Modules:
  0.0 272.6 jit_solution(11302631728159904773)
XLA Ops:
  7.3 1.1 copy.39
  8.3 11.9 %all_to_all.40 = bf16[4,1,256,128]{3,2,1,0:T(8,128)(2,1)} all-to-all(bf16[4,1,256,128]{3,2,1,0:T(8,128)(2,1)S(1)} %bitcast.68), channel_id=1, replica_groups={{0,8,16,24},{1,9,17,25},{2,10,18,26},{3,11,19,27},{4,12,20,28},{5,13,21..., dimensions={0} | all-to-all | bytes 524288 | tf_op jit(solution)/shard_map/all_to_all | solution.py:145
  20.2 0.1 all-gather.5.cloned.1.call-start
  20.3 1.0 copy.38
  21.3 8.5 %all_to_all.41 = bf16[4,1,256,128]{3,2,1,0:T(8,128)(2,1)} all-to-all(bf16[4,1,256,128]{3,2,1,0:T(8,128)(2,1)S(1)} %bitcast.69), channel_id=1, replica_groups={{0,8,16,24},{1,9,17,25},{2,10,18,26},{3,11,19,27},{4,12,20,28},{5,13,21..., dimensions={0} | all-to-all | bytes 524288 | tf_op jit(solution)/shard_map/all_to_all | solution.py:145
  29.9 2.5 copy.16
  32.4 3.6 %all-to-all-start = ((bf16[4,4,256,128]{3,2,1,0:T(8,128)(2,1)}), bf16[4,4,256,128]{3,2,1,0:T(8,128)(2,1)S(1)}, u32[]{:S(2)}, u32[]{:S(2)}) async-start(bf16[4,4,256,128]{3,2,1,0:T(8,128)(2,1)} %bitcast.2), calls=%async_computation | async-start | bytes 2097152 | tf_op jit(solution)/shard_map/all_to_all | solution.py:145
  36.0 1.2 copy.17
  37.2 10.2 %all-to-all-done.q_ref = bf16[4,4,256,128]{3,2,1,0:T(8,128)(2,1)S(1)} async-done(((bf16[4,4,256,128]{3,2,1,0:T(8,128)(2,1)}), bf16[4,4,256,128]{3,2,1,0:T(8,128)(2,1)S(1)}, u32[]{:S(2)}, u32[]{:S(2)}) %all-to-all-start) | async-done | bytes 1048608 | tf_op jit(solution)/shard_map/all_to_all | solution.py:145
  47.4 3.6 %all-to-all-start.1 = ((bf16[4,4,256,128]{3,2,1,0:T(8,128)(2,1)}), bf16[4,4,256,128]{3,2,1,0:T(8,128)(2,1)S(1)}, u32[]{:S(2)}, u32[]{:S(2)}) async-start(bf16[4,4,256,128]{3,2,1,0:T(8,128)(2,1)} %bitcast.5), calls=%async_computation.1 | async-start | bytes 2097152 | tf_op jit(solution)/shard_map/all_to_all | solution.py:145
  51.0 0.1 reduce-scatter.3.cloned.1.call-start
  51.1 3.2 %copy.20 = bf16[4,8,256,128]{3,2,1,0:T(8,128)(2,1)} copy(bf16[4,8,256,128]{3,2,0,1:T(8,128)(2,1)} %all-gather.3.cloned.1.call-done) | data formatting | bytes 4194304 | tf_op jit(solution)/shard_map/all_gather | solution.py:153
  54.3 14.7 %all-gather.5.cloned.1.call-done = bf16[4,8,256,128]{3,2,0,1:T(8,128)(2,1)} async-done(((bf16[4,1,256,128]{3,2,0,1:T(8,128)(2,1)}), bf16[4,8,256,128]{3,2,0,1:T(8,128)(2,1)}) %all-gather.5.cloned.1.call-update) | async-done | bytes 2097168 | tf_op jit(solution)/shard_map/all_gather | solution.py:154
  69.0 3.1 %copy.23 = bf16[4,8,256,128]{3,2,1,0:T(8,128)(2,1)} copy(bf16[4,8,256,128]{3,2,0,1:T(8,128)(2,1)} %all-gather.5.cloned.1.call-done) | data formatting | bytes 4194304 | tf_op jit(solution)/shard_map/all_gather | solution.py:154
  72.2 1.0 copy-done.1
  73.1 87.7 %attn_core.1 = (bf16[4,4,256,128]{3,2,1,0:T(8,128)(2,1)}, bf16[4,4,256,128]{3,2,1,0:T(8,128)(2,1)}, f32[32,256,128]{2,1,0:T(8,128)}, f32[32,256,128]{2,1,0:T(8,128)}) custom-call(bf16[4,4,256,128]{3,2,1,0:T(8,128)(2,1)} %copy-done, bf16[4,4,256,128]{3,2,1,0:T(8,128)(2,1)} %copy-done.1, bf16[32,256,128]{2,1,0:T(8,128)(2,1)} %bitcast.54, ...), custom_call_target="tpu_custom_call" | custom-call | tf_op jit(solution)/shard_map/attn_core/pallas_call | solution.py:157
  160.8 4.6 %copy.26 = f32[4,8,256,128]{3,2,0,1:T(8,128)} copy(f32[4,8,256,128]{3,2,1,0:T(8,128)} %bitcast.57) | data formatting | bytes 8388608 | tf_op jit(solution)/shard_map/reshape | solution.py:176
  165.6 4.6 %copy.28 = f32[4,8,256,128]{3,2,0,1:T(8,128)} copy(f32[4,8,256,128]{3,2,1,0:T(8,128)} %bitcast.56) | data formatting | bytes 8388608 | tf_op jit(solution)/shard_map/reshape | solution.py:176
  170.3 1.2 copy-done.3
  171.4 17.3 %all_to_all.42 = bf16[4,4,256,128]{3,2,1,0:T(8,128)(2,1)S(1)} all-to-all(bf16[4,4,256,128]{3,2,1,0:T(8,128)(2,1)S(1)} %copy-done.3), channel_id=1, replica_groups={{0,8,16,24},{1,9,17,25},{2,10,18,26},{3,11,19,27},{4,12,20,28},{5,13,21..., dimensions={0} | all-to-all | bytes 2097152 | tf_op jit(solution)/shard_map/all_to_all | solution.py:148
  188.7 3.6 %all-to-all-start.5 = ((bf16[4,4,256,128]{3,2,1,0:T(8,128)(2,1)}), bf16[4,4,256,128]{3,2,1,0:T(8,128)(2,1)S(1)}, u32[]{:S(2)}, u32[]{:S(2)}) async-start(bf16[4,4,256,128]{3,2,1,0:T(8,128)(2,1)} %get-tuple-element.9), calls=%async_computation.5 | async-start | bytes 2097152 | tf_op jit(solution)/shard_map/all_to_all | solution.py:148
  192.3 25.2 %reduce-scatter.3.cloned.1.call-done = f32[4,1,256,128]{3,2,0,1:T(8,128)} async-done(((f32[4,8,256,128]{3,2,0,1:T(8,128)}), f32[4,1,256,128]{3,2,0,1:T(8,128)}) %reduce-scatter.3.cloned.1.call-update) | async-done | bytes 524304 | tf_op jit(solution)/shard_map/reduce_scatter | solution.py:176
  217.5 1.8 fusion
  219.3 3.9 %all-to-all-start.6 = ((bf16[4,1,256,128]{3,2,1,0:T(8,128)(2,1)}), bf16[4,1,256,128]{3,2,1,0:T(8,128)(2,1)S(1)}, u32[]{:S(2)}, u32[]{:S(2)}) async-start(bf16[4,1,256,128]{3,2,1,0:T(8,128)(2,1)} %fusion), calls=%async_computation.7 | async-start | bytes 524288 | tf_op jit(solution)/shard_map/all_to_all | solution.py:148
  223.2 31.0 %reduce-scatter.5.cloned.1.call-done = f32[4,1,256,128]{3,2,0,1:T(8,128)} async-done(((f32[4,8,256,128]{3,2,0,1:T(8,128)}), f32[4,1,256,128]{3,2,0,1:T(8,128)}) %reduce-scatter.5.cloned.1.call-update) | async-done | bytes 524304 | tf_op jit(solution)/shard_map/reduce_scatter | solution.py:176
  254.2 1.8 convert_bitcast_fusion
  256.0 3.8 %all-to-all-start.7 = ((bf16[4,1,256,128]{3,2,1,0:T(8,128)(2,1)}), bf16[4,1,256,128]{3,2,1,0:T(8,128)(2,1)S(1)}, u32[]{:S(2)}, u32[]{:S(2)}) async-start(bf16[4,1,256,128]{3,2,1,0:T(8,128)(2,1)} %convert_bitcast_fusion), calls=%async_computation.9 | async-start | bytes 524288 | tf_op jit(solution)/shard_map/all_to_all | solution.py:148
  259.8 1.6 copy.37
  261.4 1.6 copy.36
  263.1 0.9 copy.30
  264.0 1.1 all-to-all-done.7
  265.1 0.9 copy.31
  (16 shorter events, 0.4 us)
Async XLA Ops:
  7.2 28.8 %copy-start.2 = (bf16[1,256,16,128]{3,2,1,0:T(8,128)(2,1)S(1)}, bf16[1,256,16,128]{3,2,1,0:T(8,128)(2,1)}, u32[]{:S(2)}) copy-start(bf16[1,256,16,128]{3,2,1,0:T(8,128)(2,1)} %param.7) | copy-start | bytes 3145732
  7.2 43.9 %all-gather.3.cloned.1.call-start = ((), (), s32[]{:S(2)}) async-start(), calls=%async_computation.10 | async-start | bytes 2359296 | tf_op jit(solution)/shard_map/all_gather | solution.py:153
  20.2 48.8 %all-gather.5.cloned.1.call-start = ((), (), s32[]{:S(2)}) async-start(), calls=%async_computation.11 | async-start | bytes 2359296 | tf_op jit(solution)/shard_map/all_gather | solution.py:154
  32.4 15.0 %all-to-all-start = ((bf16[4,4,256,128]{3,2,1,0:T(8,128)(2,1)}), bf16[4,4,256,128]{3,2,1,0:T(8,128)(2,1)S(1)}, u32[]{:S(2)}, u32[]{:S(2)}) async-start(bf16[4,4,256,128]{3,2,1,0:T(8,128)(2,1)} %bitcast.2), calls=%async_computation | async-start | bytes 2097152 | tf_op jit(solution)/shard_map/all_to_all | solution.py:145
  47.4 24.8 %copy-start = (bf16[4,4,256,128]{3,2,1,0:T(8,128)(2,1)}, bf16[4,4,256,128]{3,2,1,0:T(8,128)(2,1)S(1)}, u32[]{:S(2)}) copy-start(bf16[4,4,256,128]{3,2,1,0:T(8,128)(2,1)S(1)} %all-to-all-done.q_ref) | copy-start | bytes 3145732
  47.4 24.8 %all-to-all-start.1 = ((bf16[4,4,256,128]{3,2,1,0:T(8,128)(2,1)}), bf16[4,4,256,128]{3,2,1,0:T(8,128)(2,1)S(1)}, u32[]{:S(2)}, u32[]{:S(2)}) async-start(bf16[4,4,256,128]{3,2,1,0:T(8,128)(2,1)} %bitcast.5), calls=%async_computation.1 | async-start | bytes 2097152 | tf_op jit(solution)/shard_map/all_to_all | solution.py:145
  51.0 166.5 %reduce-scatter.3.cloned.1.call-start = ((), (), s32[]{:S(2)}) async-start(), calls=%async_computation.12 | async-start | bytes 4718592 | tf_op jit(solution)/shard_map/reduce_scatter | solution.py:176
  72.2 1.0 copy-start.1
  165.5 88.7 %reduce-scatter.5.cloned.1.call-start = ((), (), s32[]{:S(2)}) async-start(), calls=%async_computation.13 | async-start | bytes 4718592 | tf_op jit(solution)/shard_map/reduce_scatter | solution.py:176
  170.2 1.2 copy-start.3
  188.7 30.6 %all-to-all-start.5 = ((bf16[4,4,256,128]{3,2,1,0:T(8,128)(2,1)}), bf16[4,4,256,128]{3,2,1,0:T(8,128)(2,1)S(1)}, u32[]{:S(2)}, u32[]{:S(2)}) async-start(bf16[4,4,256,128]{3,2,1,0:T(8,128)(2,1)} %get-tuple-element.9), calls=%async_computation.5 | async-start | bytes 2097152 | tf_op jit(solution)/shard_map/all_to_all | solution.py:148
  219.3 36.6 %all-to-all-start.6 = ((bf16[4,1,256,128]{3,2,1,0:T(8,128)(2,1)}), bf16[4,1,256,128]{3,2,1,0:T(8,128)(2,1)S(1)}, u32[]{:S(2)}, u32[]{:S(2)}) async-start(bf16[4,1,256,128]{3,2,1,0:T(8,128)(2,1)} %fusion), calls=%async_computation.7 | async-start | bytes 524288 | tf_op jit(solution)/shard_map/all_to_all | solution.py:148
  256.0 9.1 %all-to-all-start.7 = ((bf16[4,1,256,128]{3,2,1,0:T(8,128)(2,1)}), bf16[4,1,256,128]{3,2,1,0:T(8,128)(2,1)S(1)}, u32[]{:S(2)}, u32[]{:S(2)}) async-start(bf16[4,1,256,128]{3,2,1,0:T(8,128)(2,1)} %convert_bitcast_fusion), calls=%async_computation.9 | async-start | bytes 524288 | tf_op jit(solution)/shard_map/all_to_all | solution.py:148
Sparse Core Ops, SparseCore 0:
  20.4 23.9 all-gather.2
  46.0 22.9 all-gather.4
  165.6 51.8 reduce-scatter.2
  219.7 34.4 reduce-scatter.4

commit v2 on v1

v2 whole, which is shorter than its diff:
```python
import functools

import jax
import jax.numpy as jnp
from jax import lax
from jax.experimental import pallas as pl
from jax.experimental.pallas import tpu as pltpu
from jax.sharding import PartitionSpec as P

WINDOW = 4096
NEG = -1e30
LOG2E = 1.4426950408889634
F32 = jnp.float32
BF16 = jnp.bfloat16


def dot(a, b):
    return jnp.dot(a, b, preferred_element_type=F32)


def fold8(x, op):
    n = x.shape[0] // 8
    acc = x[0:8]
    for t in range(1, n):
        acc = op(acc, x[8 * t:8 * t + 8])
    return acc


MESH = pl.DeviceIdType.MESH


def attn_kernel(inner, n_win, sm_scale, q_loc, do_loc, kv_loc, o_out, dq_out, dkv_out,
                q_all, do_all, kv_all, kt, vt, qt, dot_t, s_scr, acc_t, m_scr, l_scr, lse_scr, d_scr,
                dkv, o_st, dq_st, sib_in, x_in, dkv_st,
                loc_sem, in_s, in_r, ag_s, ag_r, sb_s, sb_r, od_s, od_r, ds_s, ds_r, xs_s, xs_r, fy_s, fy_r):
    n_y, group, chunk, dim = q_loc.shape
    n_kv = kv_all.shape[0]
    n_x = inner // 2
    half = n_kv // 2
    dp = lax.axis_index('dp')
    me = lax.axis_index('ctx')
    y, r = me // inner, lax.rem(me, inner)
    x, c = r // 2, lax.rem(r, 2)
    c_exp = sm_scale * LOG2E

    def dev(yy, xx, cc):
        return (dp, yy * inner + xx * 2 + cc)

    def y_at(dy):
        return lax.rem(y + dy + n_y, n_y)

    def x_at(dx):
        return lax.rem(x + dx + n_x, n_x)

    def rcopy(src, dst, s, rr, to):
        return pltpu.make_async_remote_copy(src_ref=src, dst_ref=dst, send_sem=s, recv_sem=rr, device_id=to, device_id_type=MESH)

    sib = dev(y, x, 1 - c)
    peers = [dev(y_at(d), x, c) for d in range(1, n_y)] + [dev(y, x_at(d), c) for d in range(1, n_x)] + [sib]
    barrier = pltpu.get_barrier_semaphore()
    for p in peers:
        pl.semaphore_signal(barrier, inc=1, device_id=p, device_id_type=MESH)
    pl.semaphore_wait(barrier, len(peers))

    mine = y * inner + r
    locs = [pltpu.make_async_copy(kv_loc.at[y], kv_all.at[mine], loc_sem.at[0]),
            pltpu.make_async_copy(q_loc.at[y], q_all.at[y], loc_sem.at[1]),
            pltpu.make_async_copy(do_loc.at[y], do_all.at[y], loc_sem.at[2])]
    for cp in locs:
        cp.start()
    order = [1, n_y - 1] + list(range(2, n_y - 1))
    ins = []
    for k, (src, dst, at) in enumerate(((kv_loc, kv_all, mine), (q_loc, q_all, y), (do_loc, do_all, y))):
        for d in order:
            cp = rcopy(src.at[y_at(d)], dst.at[at], in_s.at[k, d], in_r.at[k, d], dev(y_at(d), x, c))
            cp.start()
            ins.append(cp)

    def fwd_sib(slot, dx, idx):
        cp = rcopy(kv_all.at[idx], kv_all.at[idx], sb_s.at[slot, dx], sb_r.at[slot, dx], sib)
        cp.start()
        return cp

    xorder = [1, n_x - 1] + list(range(2, n_x - 1))
    ags, sbs = [], []
    for d in [0] + order:
        own = y_at(-d) * inner + r
        if d == 0:
            locs[0].wait()
        else:
            rcopy(kv_loc.at[y], kv_all.at[own], in_s.at[0, d], in_r.at[0, d], sib).wait_recv()
        for dx in xorder:
            cp = rcopy(kv_all.at[own], kv_all.at[own], ag_s.at[d, dx], ag_r.at[d, dx], dev(y, x_at(dx), c))
            cp.start()
            ags.append(cp)
        sbs.append(fwd_sib(d, 0, own))
    for d in [0] + order:
        for dx in xorder:
            idx = y_at(-d) * inner + x_at(-dx) * 2 + c
            rcopy(kv_all.at[idx], kv_all.at[idx], ag_s.at[d, dx], ag_r.at[d, dx], sib).wait_recv()
            sbs.append(fwd_sib(d, dx, idx))
    for d in [0] + order:
        for dx in [0] + xorder:
            idx = y_at(-d) * inner + x_at(-dx) * 2 + 1 - c
            rcopy(kv_all.at[idx], kv_all.at[idx], sb_s.at[d, dx], sb_r.at[d, dx], sib).wait_recv()
    for k, dst, loc in ((1, q_all, locs[1]), (2, do_all, locs[2])):
        loc.wait()
        for d in order:
            at = y_at(-d)
            rcopy(dst.at[at], dst.at[at], in_s.at[k, d], in_r.at[k, d], sib).wait_recv()
    for cp in ins + ags + sbs:
        cp.wait_send()

    def prep(j, _):
        kt[j] = kv_all[j, 0].T
        vt[j] = kv_all[j, 1].T
        dkv[j] = jnp.zeros((2, chunk, dim), F32)
        return 0

    lax.fori_loop(0, n_kv, prep, 0)
    rows = lax.broadcasted_iota(jnp.int32, (chunk, chunk), 0)
    cols = lax.broadcasted_iota(jnp.int32, (chunk, chunk), 1)

    def cs(h):
        return slice(h * chunk, (h + 1) * chunk)

    def out_copies(i):
        return [rcopy(st.at[i], out.at[y], od_s.at[k, i], od_r.at[k, y], dev(i, x, c))
                for k, (st, out) in enumerate(((o_st, o_out), (dq_st, dq_out)))]

    def one_chunk(step, _):
        i = n_y - 1 - step
        g = i * inner + r
        lo = jnp.maximum(g - n_win, 0)
        n = g - lo + 1
        for h in range(group):
            qt[:, cs(h)] = q_all[i, h].T
            dot_t[:, cs(h)] = do_all[i, h].T
        m_scr[...] = jnp.full(m_scr.shape, NEG, F32)
        l_scr[...] = jnp.zeros(l_scr.shape, F32)

        def score(jj, keep):
            kb = kv_all[lo + jj, 0]
            for h in range(group):
                s = dot(kb, qt[:, cs(h)])
                if keep is not None:
                    s = jnp.where(keep, s, NEG)
                s_scr[jj, :, cs(h)] = s
                m_scr[:, cs(h)] = jnp.maximum(m_scr[:, cs(h)], fold8(s, jnp.maximum))

        old_edge = g >= n_win
        first = jnp.where(old_edge, 1, 0)

        @pl.when(old_edge)
        def _():
            score(0, rows > cols)

        def score_body(jj, _):
            score(jj, None)
            return 0

        lax.fori_loop(first, n - 1, score_body, 0)
        score(n - 1, rows <= cols)
        m_row = jnp.max(m_scr[...], axis=0, keepdims=True) * c_exp
        m_scr[...] = jnp.broadcast_to(m_row, m_scr.shape)
        acc_t[...] = jnp.zeros(acc_t.shape, F32)

        def pv_body(jj, _):
            vb = vt[lo + jj]
            for h in range(group):
                p = jnp.exp2(s_scr[jj, :, cs(h)] * c_exp - m_scr[0:1, cs(h)])
                l_scr[:, cs(h)] += fold8(p, jnp.add)
                acc_t[:, cs(h)] += dot(vb, p.astype(BF16))
            return 0

        lax.fori_loop(0, n, pv_body, 0)
        l_row = jnp.sum(l_scr[...], axis=0, keepdims=True)
        lse_scr[...] = jnp.broadcast_to(m_scr[0:1] + jnp.log2(l_row), lse_scr.shape)
        for h in range(group):
            o_t = (acc_t[:, cs(h)] / l_row[:, cs(h)]).astype(BF16)
            d = jnp.sum(o_t.astype(F32) * dot_t[:, cs(h)].astype(F32), axis=0, keepdims=True)
            d_scr[:, cs(h)] = jnp.broadcast_to(d, (8, chunk))
            o_st[i, h] = o_t.T
        acc_t[...] = jnp.zeros(acc_t.shape, F32)

        @pl.when(i != y)
        def _():
            out_copies(i)[0].start()

        def bwd_body(jj, _):
            j = lo + jj
            at = lax.rem(j, 2) * half + j // 2
            vb = kv_all[j, 1]
            kb = kt[j]
            dk = dkv[at, 0]
            dv = dkv[at, 1]
            for h in range(group):
                p = jnp.exp2(s_scr[jj, :, cs(h)] * c_exp - lse_scr[0:1, cs(h)])
                dp_t = dot(vb, dot_t[:, cs(h)])
                ds = (p * (dp_t - d_scr[0:1, cs(h)])).astype(BF16)
                dv = dv + dot(p.astype(BF16), do_all[i, h])
                dk = dk + dot(ds, q_all[i, h])
                acc_t[:, cs(h)] += dot(kb, ds)
            dkv[at, 0] = dk
            dkv[at, 1] = dv
            return 0

        lax.fori_loop(0, n, bwd_body, 0)
        for h in range(group):
            dq_st[i, h] = (acc_t[:, cs(h)] * sm_scale).astype(BF16).T

        @pl.when(i != y)
        def _():
            out_copies(i)[1].start()

        return 0

    lax.fori_loop(0, n_y, one_chunk, 0)
    o_out[y] = o_st[y]
    dq_out[y] = dq_st[y]

    def sib_copy(i):
        return rcopy(dkv.at[pl.ds((1 - c) * half + n_x * i, n_x)], sib_in.at[pl.ds(n_x * i, n_x)], ds_s.at[i], ds_r.at[i], sib)

    def x_copy(i, dx):
        return rcopy(dkv.at[c * half + n_x * i + x_at(dx)], x_in.at[dx, i], xs_s.at[i, dx], xs_r.at[i, dx], dev(y, x_at(dx), c))

    def y_copy(i):
        return rcopy(dkv_st.at[i], dkv_out.at[y], fy_s.at[i], fy_r.at[y], dev(i, x, c))

    slots = list(range(n_y - 1, -1, -1))
    for i in slots:
        sib_copy(i).start()
    for i in slots:
        sib_copy(i).wait_recv()

        def add(t, _):
            at = c * half + n_x * i + t
            dkv[at] = dkv[at] + sib_in[n_x * i + t]
            return 0

        lax.fori_loop(0, n_x, add, 0)
        for dx in xorder:
            x_copy(i, dx).start()
    for i in slots:
        for dx in xorder:
            x_copy(i, dx).wait_recv()
        tot = dkv[c * half + n_x * i + x]
        for dx in xorder:
            tot = tot + x_in[dx, i]
        dkv_st[i, 0] = (tot[0] * sm_scale).astype(BF16)
        dkv_st[i, 1] = tot[1].astype(BF16)

        @pl.when(i != y)
        def _():
            y_copy(i).start()

    dkv_out[y] = dkv_st[y]
    for yy in range(n_y):
        @pl.when(yy != y)
        def _():
            for k, out in enumerate((o_out, dq_out)):
                rcopy(o_st.at[yy], out.at[yy], od_s.at[k, yy], od_r.at[k, yy], sib).wait_recv()
            rcopy(dkv_st.at[yy], dkv_out.at[yy], fy_s.at[yy], fy_r.at[yy], sib).wait_recv()
            for cp in out_copies(yy):
                cp.wait_send()
            y_copy(yy).wait_send()

        sib_copy(yy).wait_send()
        for dx in xorder:
            x_copy(yy, dx).wait_send()


def solution(mesh):
    n_ctx = mesh.shape['ctx']
    seq_spec = P('dp', 'ctx', None, None)

    def local_attn(q_loc, k_loc, v_loc, do_loc):
        n_batch, chunk, q_heads, dim = q_loc.shape
        kv_heads = k_loc.shape[2]
        group = q_heads // kv_heads
        inner = n_ctx // kv_heads
        n_x = inner // 2
        n_win = WINDOW // chunk
        n_y = kv_heads
        wide = group * chunk

        def heads(x, per):
            return jnp.transpose(x[0], (1, 0, 2)).reshape(kv_heads, per, chunk, dim)

        def tokens(x):
            return jnp.transpose(x.reshape(-1, chunk, dim), (1, 0, 2))[None]

        q4, do4 = heads(q_loc, group), heads(do_loc, group)
        kv4 = jnp.concatenate([heads(k_loc, 1), heads(v_loc, 1)], axis=1)
        vm = pl.BlockSpec(memory_space=pltpu.VMEM)
        dma = pltpu.SemaphoreType.DMA
        o4, dq4, dkv4 = pl.pallas_call(
            functools.partial(attn_kernel, inner, n_win, dim ** -0.5),
            out_shape=(jax.ShapeDtypeStruct(q4.shape, BF16), jax.ShapeDtypeStruct(q4.shape, BF16),
                       jax.ShapeDtypeStruct(kv4.shape, BF16)),
            in_specs=[vm] * 3,
            out_specs=(vm,) * 3,
            scratch_shapes=[
                pltpu.VMEM(q4.shape, BF16), pltpu.VMEM(q4.shape, BF16), pltpu.VMEM((n_ctx, 2, chunk, dim), BF16),
                pltpu.VMEM((n_ctx, dim, chunk), BF16), pltpu.VMEM((n_ctx, dim, chunk), BF16),
                pltpu.VMEM((dim, wide), BF16), pltpu.VMEM((dim, wide), BF16),
                pltpu.VMEM((n_win + 1, chunk, wide), F32), pltpu.VMEM((dim, wide), F32),
                pltpu.VMEM((8, wide), F32), pltpu.VMEM((8, wide), F32),
                pltpu.VMEM((8, wide), F32), pltpu.VMEM((8, wide), F32),
                pltpu.VMEM((n_ctx, 2, chunk, dim), F32), pltpu.VMEM(q4.shape, BF16), pltpu.VMEM(q4.shape, BF16),
                pltpu.VMEM((n_ctx // 2, 2, chunk, dim), F32), pltpu.VMEM((n_x, n_y, 2, chunk, dim), F32),
                pltpu.VMEM(kv4.shape, BF16),
                dma((3,)), dma((3, n_y)), dma((3, n_y)), dma((n_y, n_x)), dma((n_y, n_x)), dma((n_y, n_x)), dma((n_y, n_x)),
                dma((2, n_y)), dma((2, n_y)), dma((n_y,)), dma((n_y,)), dma((n_y, n_x)), dma((n_y, n_x)),
                dma((n_y,)), dma((n_y,)),
            ],
            compiler_params=pltpu.CompilerParams(vmem_limit_bytes=63 * 1024 * 1024, collective_id=0, has_side_effects=True),
            name='attn_core',
        )(q4, do4, kv4)
        return tokens(o4), tokens(dq4), tokens(dkv4[:, 0]), tokens(dkv4[:, 1])

    return jax.shard_map(local_attn, mesh=mesh, in_specs=(seq_spec,) * 4, out_specs=(seq_spec,) * 4, check_vma=False)
```

time: 276 us -> 209 us (0.76); the launches traced: 273 us -> 208 us
  Pallas kernels: 87.7 us -> 197 us
  waiting for transfers between devices: 82.4 us -> 0 us
  blocking collectives: 37.6 us -> 0 us
  starting transfers between devices: 18.8 us -> 0 us
  local copies, waits for them, and re-layouts: 28.6 us -> 10.2 us
  between operations: 13.9 us -> 0.67 us
    pallas_call x1, Pallas kernels: 87.7 us -> 197 us  [local_attn(): pl.pallas_call(functools.partial(attn_kernel, inner, n_win, dim ** (-0.5)...]
    reduce_scatter x2 -> x0, waiting for transfers between devices: 56.2 us -> none  [reduce(): lax.psum_scatter(x.reshape(n_q, inner, chunk, dim), 'ctx', scatter_dimens...]
    all_to_all x3 -> x0, blocking collectives: 37.6 us -> none  [the longest x2 20.4 us: split(): return lax.all_to_all(x, 'ctx', 0, 0, axis_index_groups=cols)]
    all_to_all x5 -> x0, starting transfers between devices: 18.5 us -> none  [the longest x3 11.3 us: merge(): x = lax.all_to_all(x, 'ctx', 0, 0, axis_index_groups=cols)]
    all_gather x2 -> x0, waiting for transfers between devices: 14.7 us -> none  [the longest x1 14.7 us: local_attn(): lax.all_gather(v4[:, 0], 'ctx', axis_index_groups=rows, axis=1)]
    all_to_all x5 -> x0, waiting for transfers between devices: 11.3 us -> none  [the longest x2 10.2 us: split(): return lax.all_to_all(x, 'ctx', 0, 0, axis_index_groups=cols)]
    reshape x4 -> x3, local copies, waits for them, and re-layouts: 12.5 us -> 5.8 us  [the longest x2 4.61 us: tokens(): return jnp.transpose(x.reshape(-1, chunk, dim), (1, 0, 2))[None]]
    all_gather x2 -> x0, local copies, waits for them, and re-layouts: 6.36 us -> none  [the longest x1 3.21 us: local_attn(): lax.all_gather(k4[:, 0], 'ctx', axis_index_groups=rows, axis=1)]
  transfers between devices with their start and end apart: 9 -> 0, of which waited for: 5 -> 0; matrix products, arithmetic and copies ran while one was open for 9% -> 0% of each run, Pallas kernels for 0% -> 0%
where the time goes in v2:
time: 209 us; the launch traced here: 208 us
  Pallas kernels  197 us (94%)
  local copies, waits for them, and re-layouts  10.2 us (5%)
    pallas_call x1, Pallas kernels, local_attn(): pl.pallas_call(functools.partial(attn_kernel, inner, n_win, dim ** (-0.5)...  197 us
    reshape x2, local copies, waits for them, and re-layouts, tokens(): return jnp.transpose(x.reshape(-1, chunk, dim), (1, 0, 2))[None]  4.61 us

profile of v2, /device:TPU:97, one launch (start us, length us, event | category | flops | bytes accessed | tf_op | source)
XLA Modules:
  0.0 208.4 jit_solution(17898351242143886060)
XLA Ops:
  0.6 0.0 copy-start
  0.6 1.2 copy_bitcast_fusion.2
  1.8 0.9 pad_maximum_fusion.kv_loc
  2.7 0.0 copy-done
  2.7 0.0 copy-start.1
  2.7 1.2 copy.8
  3.9 0.1 copy-done.1
  4.0 1.2 copy.9
  5.2 196.6 %attn_core.1 = (bf16[4,4,256,128]{3,2,1,0:T(8,128)(2,1)}, bf16[4,4,256,128]{3,2,1,0:T(8,128)(2,1)}, bf16[4,2,256,128]{3,2,1,0:T(8,128)(2,1)}) custom-call(bf16[4,4,256,128]{3,2,1,0:T(8,128)(2,1)} %bitcast.44, bf16[4,4,256,128]{3,2,1,0:T(8,128)(2,1)} %bitcast.45, bf16[4,2,256,128]{3,2,1,0:T(8,128)(2,1)} %pad_maximum_fusion.kv_loc), custom_call_target="tpu_custom_call" | custom-call | tf_op jit(solution)/shard_map/attn_core/pallas_call | solution.py:298
  201.9 0.0 copy-start.2
  201.9 3.0 %copy.21 = bf16[16,256,128]{2,0,1:T(8,128)(2,1)} copy(bf16[16,256,128]{2,1,0:T(8,128)(2,1)} %bitcast.51) | data formatting | bytes 2097152 | tf_op jit(solution)/shard_map/reshape | solution.py:292
  204.8 0.0 copy-done.2
  204.8 0.0 copy-start.3
  204.8 1.6 copy.20
  206.5 0.0 copy-done.3
  206.5 0.9 copy.15
  207.4 0.9 copy.14
  (1 shorter events, 0.0 us)
Async XLA Ops:
  0.6 2.1 copy-start
  2.7 1.3 copy-start.1
  201.9 3.0 %copy-start.2 = (bf16[4,4,256,128]{3,2,1,0:T(8,128)(2,1)S(1)}, bf16[4,4,256,128]{3,2,1,0:T(8,128)(2,1)}, u32[]{:S(2)}) copy-start(bf16[4,4,256,128]{3,2,1,0:T(8,128)(2,1)} %get-tuple-element.8) | copy-start | bytes 3145732
  204.8 1.7 copy-start.3

commit v3 on v2

--- a/solution.py
+++ b/solution.py
@@ -138,42 +138,60 @@
             dot_t[:, cs(h)] = do_all[i, h].T
         m_scr[...] = jnp.full(m_scr.shape, NEG, F32)
         l_scr[...] = jnp.zeros(l_scr.shape, F32)
-
-        def score(jj, keep):
-            kb = kv_all[lo + jj, 0]
+        acc_t[...] = jnp.zeros(acc_t.shape, F32)
+
+        def fwd(blocks):
+            def score(h):
+                return [dot(kv_all[lo + jj, 0], qt[:, cs(h)]) for jj, _ in blocks]
+
+            nxt = score(0)
             for h in range(group):
-                s = dot(kb, qt[:, cs(h)])
-                if keep is not None:
-                    s = jnp.where(keep, s, NEG)
-                s_scr[jj, :, cs(h)] = s
-                m_scr[:, cs(h)] = jnp.maximum(m_scr[:, cs(h)], fold8(s, jnp.maximum))
+                cur = nxt
+                if h + 1 < group:
+                    nxt = score(h + 1)
+                m_old = m_scr[:, cs(h)]
+                mx = m_old
+                for (jj, keep), s in zip(blocks, cur):
+                    s = s * c_exp
+                    if keep is not None:
+                        s = jnp.where(keep, s, NEG)
+                    s_scr[jj, :, cs(h)] = s
+                    mx = jnp.maximum(mx, fold8(s, jnp.maximum))
+                m_new = jnp.broadcast_to(jnp.max(mx, axis=0, keepdims=True), m_old.shape)
+                alpha = jnp.exp2(m_old - m_new)
+                m_scr[:, cs(h)] = m_new
+                l_new = l_scr[:, cs(h)] * alpha
+                pv = None
+                for jj, _ in blocks:
+                    p = jnp.exp2(s_scr[jj, :, cs(h)] - m_new[0:1])
+                    l_new = l_new + fold8(p, jnp.add)
+                    part = dot(vt[lo + jj], p.astype(BF16))
+                    pv = part if pv is None else pv + part
+                l_scr[:, cs(h)] = l_new
+                acc_t[:, cs(h)] = acc_t[:, cs(h)] * alpha[0:1] + pv
 
         old_edge = g >= n_win
         first = jnp.where(old_edge, 1, 0)
+        n_mid = n - 1 - first
 
         @pl.when(old_edge)
         def _():
-            score(0, rows > cols)
-
-        def score_body(jj, _):
-            score(jj, None)
+            fwd([(0, rows > cols), (n - 1, rows <= cols)])
+
+        @pl.when(jnp.logical_not(old_edge))
+        def _():
+            fwd([(n - 1, rows <= cols)])
+
+        def fwd_body(t, _):
+            fwd([(first + 2 * t, None), (first + 2 * t + 1, None)])
             return 0
 
-        lax.fori_loop(first, n - 1, score_body, 0)
-        score(n - 1, rows <= cols)
-        m_row = jnp.max(m_scr[...], axis=0, keepdims=True) * c_exp
-        m_scr[...] = jnp.broadcast_to(m_row, m_scr.shape)
-        acc_t[...] = jnp.zeros(acc_t.shape, F32)
-
-        def pv_body(jj, _):
-            vb = vt[lo + jj]
-            for h in range(group):
-                p = jnp.exp2(s_scr[jj, :, cs(h)] * c_exp - m_scr[0:1, cs(h)])
-                l_scr[:, cs(h)] += fold8(p, jnp.add)
-                acc_t[:, cs(h)] += dot(vb, p.astype(BF16))
-            return 0
-
-        lax.fori_loop(0, n, pv_body, 0)
+        lax.fori_loop(0, n_mid // 2, fwd_body, 0)
+
+        @pl.when(lax.rem(n_mid, 2) == 1)
+        def _():
+            fwd([(first + n_mid - 1, None)])
+
         l_row = jnp.sum(l_scr[...], axis=0, keepdims=True)
         lse_scr[...] = jnp.broadcast_to(m_scr[0:1] + jnp.log2(l_row), lse_scr.shape)
         for h in range(group):
@@ -187,25 +205,41 @@
         def _():
             out_copies(i)[0].start()
 
-        def bwd_body(jj, _):
-            j = lo + jj
-            at = lax.rem(j, 2) * half + j // 2
-            vb = kv_all[j, 1]
-            kb = kt[j]
-            dk = dkv[at, 0]
-            dv = dkv[at, 1]
-            for h in range(group):
-                p = jnp.exp2(s_scr[jj, :, cs(h)] * c_exp - lse_scr[0:1, cs(h)])
-                dp_t = dot(vb, dot_t[:, cs(h)])
-                ds = (p * (dp_t - d_scr[0:1, cs(h)])).astype(BF16)
-                dv = dv + dot(p.astype(BF16), do_all[i, h])
-                dk = dk + dot(ds, q_all[i, h])
-                acc_t[:, cs(h)] += dot(kb, ds)
-            dkv[at, 0] = dk
-            dkv[at, 1] = dv
+        def bwd(jjs):
+            units = [(b, h) for b in range(len(jjs)) for h in range(group)]
+            at_j = [lo + jj for jj in jjs]
+            at = [lax.rem(j, 2) * half + j // 2 for j in at_j]
+
+            def grad_p(b, h):
+                return dot(kv_all[at_j[b], 1], dot_t[:, cs(h)])
+
+            nxt = grad_p(*units[0])
+            dk = dv = None
+            for k, (b, h) in enumerate(units):
+                cur = nxt
+                if k + 1 < len(units):
+                    nxt = grad_p(*units[k + 1])
+                p = jnp.exp2(s_scr[jjs[b], :, cs(h)] - lse_scr[0:1, cs(h)])
+                ds = (p * (cur - d_scr[0:1, cs(h)])).astype(BF16)
+                part = dot(p.astype(BF16), do_all[i, h])
+                dv = part if h == 0 else dv + part
+                part = dot(ds, q_all[i, h])
+                dk = part if h == 0 else dk + part
+                acc_t[:, cs(h)] += dot(kt[at_j[b]], ds)
+                if h == group - 1:
+                    dkv[at[b], 0] += dk
+                    dkv[at[b], 1] += dv
+
+        def bwd_body(t, _):
+            bwd([2 * t, 2 * t + 1])
             return 0
 
-        lax.fori_loop(0, n, bwd_body, 0)
+        lax.fori_loop(0, n // 2, bwd_body, 0)
+
+        @pl.when(lax.rem(n, 2) == 1)
+        def _():
+            bwd([n - 1])
+
         for h in range(group):
             dq_st[i, h] = (acc_t[:, cs(h)] * sm_scale).astype(BF16).T
 

time: 209 us -> 179 us (0.86)
  Pallas kernels: 197 us -> 168 us
    pallas_call x1, Pallas kernels: 197 us -> 168 us  [local_attn(): pl.pallas_call(functools.partial(attn_kernel, inner, n_win, dim ** (-0.5)...]
where the time goes in v3:
time: 179 us
  Pallas kernels  168 us (94%)
  local copies, waits for them, and re-layouts  10.2 us (6%)
    pallas_call x1, Pallas kernels, local_attn(): pl.pallas_call(functools.partial(attn_kernel, inner, n_win, dim ** (-0.5)...  168 us
    reshape x2, local copies, waits for them, and re-layouts, tokens(): return jnp.transpose(x.reshape(-1, chunk, dim), (1, 0, 2))[None]  4.61 us

profile of v3, /device:TPU:97, one launch (start us, length us, event | category | flops | bytes accessed | tf_op | source)
XLA Modules:
  0.0 179.2 jit_solution(13550715241071113767)
XLA Ops:
  0.6 0.0 copy-start
  0.6 1.2 copy_bitcast_fusion.2
  1.8 0.9 pad_maximum_fusion.kv_loc
  2.7 0.0 copy-done
  2.7 0.0 copy-start.1
  2.7 1.2 copy.8
  3.9 0.1 copy-done.1
  4.0 1.2 copy.9
  5.2 167.5 %attn_core.1 = (bf16[4,4,256,128]{3,2,1,0:T(8,128)(2,1)}, bf16[4,4,256,128]{3,2,1,0:T(8,128)(2,1)}, bf16[4,2,256,128]{3,2,1,0:T(8,128)(2,1)}) custom-call(bf16[4,4,256,128]{3,2,1,0:T(8,128)(2,1)} %bitcast.44, bf16[4,4,256,128]{3,2,1,0:T(8,128)(2,1)} %bitcast.45, bf16[4,2,256,128]{3,2,1,0:T(8,128)(2,1)} %pad_maximum_fusion.kv_loc), custom_call_target="tpu_custom_call" | custom-call | tf_op jit(solution)/shard_map/attn_core/pallas_call | solution.py:332
  172.7 0.0 copy-start.2
  172.7 3.0 %copy.21 = bf16[16,256,128]{2,0,1:T(8,128)(2,1)} copy(bf16[16,256,128]{2,1,0:T(8,128)(2,1)} %bitcast.51) | data formatting | bytes 2097152 | tf_op jit(solution)/shard_map/reshape | solution.py:326
  175.7 0.0 copy-done.2
  175.7 0.0 copy-start.3
  175.7 1.6 copy.20
  177.4 0.0 copy-done.3
  177.4 0.9 copy.15
  178.3 0.9 copy.14
  (1 shorter events, 0.0 us)
Async XLA Ops:
  0.6 2.1 %copy-start = (bf16[1,256,16,128]{3,2,1,0:T(8,128)(2,1)S(1)}, bf16[1,256,16,128]{3,2,1,0:T(8,128)(2,1)}, u32[]{:S(2)}) copy-start(bf16[1,256,16,128]{3,2,1,0:T(8,128)(2,1)} %param.4) | copy-start | bytes 3145732
  2.7 1.3 copy-start.1
  172.7 3.0 %copy-start.2 = (bf16[4,4,256,128]{3,2,1,0:T(8,128)(2,1)S(1)}, bf16[4,4,256,128]{3,2,1,0:T(8,128)(2,1)}, u32[]{:S(2)}) copy-start(bf16[4,4,256,128]{3,2,1,0:T(8,128)(2,1)} %get-tuple-element.8) | copy-start | bytes 3145732
  175.7 1.7 copy-start.3

commit v4 on v3

--- a/solution.py
+++ b/solution.py
@@ -127,6 +127,40 @@
     def out_copies(i):
         return [rcopy(st.at[i], out.at[y], od_s.at[k, i], od_r.at[k, y], dev(i, x, c))
                 for k, (st, out) in enumerate(((o_st, o_out), (dq_st, dq_out)))]
+
+    def sib_copy(i):
+        return rcopy(dkv.at[pl.ds((1 - c) * half + n_x * i, n_x)], sib_in.at[pl.ds(n_x * i, n_x)], ds_s.at[i], ds_r.at[i], sib)
+
+    def x_copy(i, dx):
+        return rcopy(dkv.at[c * half + n_x * i + x_at(dx)], x_in.at[dx, i], xs_s.at[i, dx], xs_r.at[i, dx], dev(y, x_at(dx), c))
+
+    def y_copy(i):
+        return rcopy(dkv_st.at[i], dkv_out.at[y], fy_s.at[i], fy_r.at[y], dev(i, x, c))
+
+    def reduce_start(i):
+        sib_copy(i).wait_recv()
+
+        def add(t, _):
+            at = c * half + n_x * i + t
+            dkv[at] = dkv[at] + sib_in[n_x * i + t]
+            return 0
+
+        lax.fori_loop(0, n_x, add, 0)
+        for dx in xorder:
+            x_copy(i, dx).start()
+
+    def reduce_end(i):
+        for dx in xorder:
+            x_copy(i, dx).wait_recv()
+        tot = dkv[c * half + n_x * i + x]
+        for dx in xorder:
+            tot = tot + x_in[dx, i]
+        dkv_st[i, 0] = (tot[0] * sm_scale).astype(BF16)
+        dkv_st[i, 1] = tot[1].astype(BF16)
+
+        @pl.when(i != y)
+        def _():
+            y_copy(i).start()
 
     def one_chunk(step, _):
         i = n_y - 1 - step
@@ -205,6 +239,10 @@
         def _():
             out_copies(i)[0].start()
 
+        @pl.when(step > 0)
+        def _():
+            reduce_start(i + 1)
+
         def bwd(jjs):
             units = [(b, h) for b in range(len(jjs)) for h in range(group)]
             at_j = [lo + jj for jj in jjs]
@@ -247,47 +285,19 @@
         def _():
             out_copies(i)[1].start()
 
+        sib_copy(i).start()
+
+        @pl.when(step > 0)
+        def _():
+            reduce_end(i + 1)
+
         return 0
 
     lax.fori_loop(0, n_y, one_chunk, 0)
+    reduce_start(0)
     o_out[y] = o_st[y]
     dq_out[y] = dq_st[y]
-
-    def sib_copy(i):
-        return rcopy(dkv.at[pl.ds((1 - c) * half + n_x * i, n_x)], sib_in.at[pl.ds(n_x * i, n_x)], ds_s.at[i], ds_r.at[i], sib)
-
-    def x_copy(i, dx):
-        return rcopy(dkv.at[c * half + n_x * i + x_at(dx)], x_in.at[dx, i], xs_s.at[i, dx], xs_r.at[i, dx], dev(y, x_at(dx), c))
-
-    def y_copy(i):
-        return rcopy(dkv_st.at[i], dkv_out.at[y], fy_s.at[i], fy_r.at[y], dev(i, x, c))
-
-    slots = list(range(n_y - 1, -1, -1))
-    for i in slots:
-        sib_copy(i).start()
-    for i in slots:
-        sib_copy(i).wait_recv()
-
-        def add(t, _):
-            at = c * half + n_x * i + t
-            dkv[at] = dkv[at] + sib_in[n_x * i + t]
-            return 0
-
-        lax.fori_loop(0, n_x, add, 0)
-        for dx in xorder:
-            x_copy(i, dx).start()
-    for i in slots:
-        for dx in xorder:
-            x_copy(i, dx).wait_recv()
-        tot = dkv[c * half + n_x * i + x]
-        for dx in xorder:
-            tot = tot + x_in[dx, i]
-        dkv_st[i, 0] = (tot[0] * sm_scale).astype(BF16)
-        dkv_st[i, 1] = tot[1].astype(BF16)
-
-        @pl.when(i != y)
-        def _():
-            y_copy(i).start()
+    reduce_end(0)
 
     dkv_out[y] = dkv_st[y]
     for yy in range(n_y):

time: 179 us -> 149 us (0.83); the launches traced: 179 us -> 147 us
  Pallas kernels: 168 us -> 135 us
    pallas_call x1, Pallas kernels: 168 us -> 135 us  [local_attn(): pl.pallas_call(functools.partial(attn_kernel, inner, n_win, dim ** (-0.5)...]
where the time goes in v4:
time: 149 us; the launch traced here: 147 us
  Pallas kernels  135 us (91%)
  local copies, waits for them, and re-layouts  10.2 us (7%)
    pallas_call x1, Pallas kernels, local_attn(): pl.pallas_call(functools.partial(attn_kernel, inner, n_win, dim ** (-0.5)...  135 us
    reshape x2, local copies, waits for them, and re-layouts, tokens(): return jnp.transpose(x.reshape(-1, chunk, dim), (1, 0, 2))[None]  4.61 us

profile of v4, /device:TPU:97, one launch (start us, length us, event | category | flops | bytes accessed | tf_op | source)
XLA Modules:
  0.0 146.7 jit_solution(12718713498847994279)
XLA Ops:
  0.6 0.0 copy-start
  0.6 1.2 copy_bitcast_fusion.2
  1.8 0.9 pad_maximum_fusion.kv_loc
  2.7 0.0 copy-done
  2.7 0.0 copy-start.1
  2.7 1.2 copy.8
  3.9 0.1 copy-done.1
  4.0 1.2 copy.9
  5.2 135.0 %attn_core.1 = (bf16[4,4,256,128]{3,2,1,0:T(8,128)(2,1)}, bf16[4,4,256,128]{3,2,1,0:T(8,128)(2,1)}, bf16[4,2,256,128]{3,2,1,0:T(8,128)(2,1)}) custom-call(bf16[4,4,256,128]{3,2,1,0:T(8,128)(2,1)} %bitcast.44, bf16[4,4,256,128]{3,2,1,0:T(8,128)(2,1)} %bitcast.45, bf16[4,2,256,128]{3,2,1,0:T(8,128)(2,1)} %pad_maximum_fusion.kv_loc), custom_call_target="tpu_custom_call" | custom-call | tf_op jit(solution)/shard_map/attn_core/pallas_call | solution.py:342
  140.2 0.0 copy-start.2
  140.2 3.0 %copy.21 = bf16[16,256,128]{2,0,1:T(8,128)(2,1)} copy(bf16[16,256,128]{2,1,0:T(8,128)(2,1)} %bitcast.51) | data formatting | bytes 2097152 | tf_op jit(solution)/shard_map/reshape | solution.py:336
  143.2 0.0 copy-done.2
  143.2 0.0 copy-start.3
  143.2 1.6 %copy.20 = bf16[16,256,128]{2,0,1:T(8,128)(2,1)} copy(bf16[16,256,128]{2,1,0:T(8,128)(2,1)S(1)} %bitcast.50) | data formatting | bytes 2097152 | tf_op jit(solution)/shard_map/reshape | solution.py:336
  144.9 0.0 copy-done.3
  144.9 0.9 copy.15
  145.8 0.9 copy.14
  (1 shorter events, 0.0 us)
Async XLA Ops:
  0.6 2.1 %copy-start = (bf16[1,256,16,128]{3,2,1,0:T(8,128)(2,1)S(1)}, bf16[1,256,16,128]{3,2,1,0:T(8,128)(2,1)}, u32[]{:S(2)}) copy-start(bf16[1,256,16,128]{3,2,1,0:T(8,128)(2,1)} %param.4) | copy-start | bytes 3145732
  2.7 1.3 copy-start.1
  140.2 3.0 %copy-start.2 = (bf16[4,4,256,128]{3,2,1,0:T(8,128)(2,1)S(1)}, bf16[4,4,256,128]{3,2,1,0:T(8,128)(2,1)}, u32[]{:S(2)}) copy-start(bf16[4,4,256,128]{3,2,1,0:T(8,128)(2,1)} %get-tuple-element.8) | copy-start | bytes 3145732
  143.2 1.7 %copy-start.3 = (bf16[4,2,256,128]{3,2,1,0:T(8,128)(2,1)S(1)}, bf16[4,2,256,128]{3,2,1,0:T(8,128)(2,1)}, u32[]{:S(2)}) copy-start(bf16[4,2,256,128]{3,2,1,0:T(8,128)(2,1)} %get-tuple-element.9) | copy-start | bytes 1572868

commit v5 on v4

v5 whole, which is shorter than its diff:
```python
import functools

import jax
import jax.numpy as jnp
from jax import lax
from jax.experimental import pallas as pl
from jax.experimental.pallas import tpu as pltpu
from jax.sharding import PartitionSpec as P

WINDOW = 4096
NEG = -1e30
LOG2E = 1.4426950408889634
F32 = jnp.float32
BF16 = jnp.bfloat16


def dot(a, b):
    return jnp.dot(a, b, preferred_element_type=F32)


def fold8(x, op):
    n = x.shape[0] // 8
    acc = x[0:8]
    for t in range(1, n):
        acc = op(acc, x[8 * t:8 * t + 8])
    return acc


MESH = pl.DeviceIdType.MESH


def attn_kernel(inner, n_win, sm_scale, q_loc, do_loc, kv_loc, o_out, dq_out, dkv_out,
                q_all, do_all, kv_all, kt, vt, qt, dot_t, s_scr, acc_t, m_scr, l_scr, lse_scr, d_scr,
                p_a, s_a, p_b, s_b, dkv, o_st, dq_st, sib_in, x_in, dkv_st,
                loc_sem, in_s, in_r, ag_s, ag_r, sb_s, sb_r, od_s, od_r, ds_s, ds_r, xs_s, xs_r, fy_s, fy_r):
    n_y, group, chunk, dim = q_loc.shape
    n_kv = kv_all.shape[0]
    n_x = inner // 2
    half = n_kv // 2
    top = n_y - 1
    dp = lax.axis_index('dp')
    me = lax.axis_index('ctx')
    y, r = me // inner, lax.rem(me, inner)
    x, c = r // 2, lax.rem(r, 2)
    c_exp = sm_scale * LOG2E

    def dev(yy, xx, cc):
        return (dp, yy * inner + xx * 2 + cc)

    def y_at(dy):
        return lax.rem(y + dy + n_y, n_y)

    def x_at(dx):
        return lax.rem(x + dx + n_x, n_x)

    def rcopy(src, dst, s, rr, to):
        return pltpu.make_async_remote_copy(src_ref=src, dst_ref=dst, send_sem=s, recv_sem=rr, device_id=to, device_id_type=MESH)

    sib = dev(y, x, 1 - c)
    peers = [dev(y_at(d), x, c) for d in range(1, n_y)] + [dev(y, x_at(d), c) for d in range(1, n_x)] + [sib]
    barrier = pltpu.get_barrier_semaphore()
    for p in peers:
        pl.semaphore_signal(barrier, inc=1, device_id=p, device_id_type=MESH)
    pl.semaphore_wait(barrier, len(peers))

    yorder = [1, n_y - 1] + list(range(2, n_y - 1))
    xorder = [1, n_x - 1] + list(range(2, n_x - 1))
    mine = y * inner + r
    locs = [pltpu.make_async_copy(kv_loc.at[y], kv_all.at[mine], loc_sem.at[0]),
            pltpu.make_async_copy(q_loc.at[y], q_all.at[y], loc_sem.at[1]),
            pltpu.make_async_copy(do_loc.at[y], do_all.at[y], loc_sem.at[2])]
    for cp in locs:
        cp.start()

    def kv_copy(d):
        return rcopy(kv_loc.at[y_at(d)], kv_all.at[mine], in_s.at[0, d], in_r.at[0, d], dev(y_at(d), x, c))

    def qdo_copies(d):
        return [rcopy(src.at[y_at(d)], dst.at[y], in_s.at[k, d], in_r.at[k, d], dev(y_at(d), x, c))
                for k, src, dst in ((1, q_loc, q_all), (2, do_loc, do_all))]

    def send_qdo():
        for d in yorder:
            for cp in qdo_copies(d):
                cp.start()

    def wait_qdo(s):
        @pl.when(s != y)
        def _():
            d = y_at(-s)
            for k, dst in ((1, q_all), (2, do_all)):
                rcopy(dst.at[s], dst.at[s], in_s.at[k, d], in_r.at[k, d], sib).wait_recv()

    def ag_copy(s, dx):
        idx = s * inner + r
        return rcopy(kv_all.at[idx], kv_all.at[idx], ag_s.at[s, dx], ag_r.at[s, dx], dev(y, x_at(dx), c))

    def sb_copy(s, dx):
        idx = s * inner + x_at(-dx) * 2 + c
        return rcopy(kv_all.at[idx], kv_all.at[idx], sb_s.at[s, dx], sb_r.at[s, dx], sib)

    for d in yorder:
        kv_copy(d).start()

    @pl.when(y == top)
    def _():
        send_qdo()

    slots = list(range(top, -1, -1))
    for s in slots:
        idx = s * inner + r

        @pl.when(s == y)
        def _():
            locs[0].wait()

        @pl.when(s != y)
        def _():
            d = y_at(-s)
            rcopy(kv_all.at[idx], kv_all.at[idx], in_s.at[0, d], in_r.at[0, d], sib).wait_recv()

        for dx in xorder:
            ag_copy(s, dx).start()
        sb_copy(s, 0).start()

    def ready(s):
        for dx in xorder:
            idx = s * inner + x_at(-dx) * 2 + c
            rcopy(kv_all.at[idx], kv_all.at[idx], ag_s.at[s, dx], ag_r.at[s, dx], sib).wait_recv()
            sb_copy(s, dx).start()
        for dx in [0] + xorder:
            idx = s * inner + x_at(-dx) * 2 + 1 - c
            rcopy(kv_all.at[idx], kv_all.at[idx], sb_s.at[s, dx], sb_r.at[s, dx], sib).wait_recv()

        def prep(t, _):
            j = s * inner + t
            kt[j] = kv_all[j, 0].T
            vt[j] = kv_all[j, 1].T
            dkv[lax.rem(j, 2) * half + j // 2] = jnp.zeros((2, chunk, dim), F32)
            return 0

        lax.fori_loop(0, inner, prep, 0)

    ready(top)

    @pl.when(r == 0)
    def _():
        ready(top - 1)

    locs[1].wait()
    locs[2].wait()
    wait_qdo(top)

    @pl.when(y != top)
    def _():
        send_qdo()

    need_1 = (r + 1) // 2
    need_2 = (r + inner + 1) // 2
    diff = lax.broadcasted_iota(jnp.int32, (chunk, chunk), 0) - lax.broadcasted_iota(jnp.int32, (chunk, chunk), 1)

    def cs(h):
        return slice(h * chunk, (h + 1) * chunk)

    def out_copies(i):
        return [rcopy(st.at[i], out.at[y], od_s.at[k, i], od_r.at[k, y], dev(i, x, c))
                for k, (st, out) in enumerate(((o_st, o_out), (dq_st, dq_out)))]

    def sib_copy(i):
        return rcopy(dkv.at[pl.ds((1 - c) * half + n_x * i, n_x)], sib_in.at[pl.ds(n_x * i, n_x)], ds_s.at[i], ds_r.at[i], sib)

    def x_copy(i, dx):
        return rcopy(dkv.at[c * half + n_x * i + x_at(dx)], x_in.at[dx, i], xs_s.at[i, dx], xs_r.at[i, dx], dev(y, x_at(dx), c))

    def y_copy(i):
        return rcopy(dkv_st.at[i], dkv_out.at[y], fy_s.at[i], fy_r.at[y], dev(i, x, c))

    def reduce_start(i):
        sib_copy(i).wait_recv()

        def add(t, _):
            at = c * half + n_x * i + t
            dkv[at] = dkv[at] + sib_in[n_x * i + t]
            return 0

        lax.fori_loop(0, n_x, add, 0)
        for dx in xorder:
            x_copy(i, dx).start()

    def reduce_end(i):
        for dx in xorder:
            x_copy(i, dx).wait_recv()
        tot = dkv[c * half + n_x * i + x]
        for dx in xorder:
            tot = tot + x_in[dx, i]
        dkv_st[i, 0] = (tot[0] * sm_scale).astype(BF16)
        dkv_st[i, 1] = tot[1].astype(BF16)

        @pl.when(i != y)
        def _():
            y_copy(i).start()

    def one_chunk(step, _):
        i = top - step
        g = i * inner + r
        n = jnp.maximum(jnp.minimum(g, n_win) + 1, 2)
        for h in range(group):
            qt[:, cs(h)] = q_all[i, h].T
            dot_t[:, cs(h)] = do_all[i, h].T
        m_scr[...] = jnp.full(m_scr.shape, NEG, F32)
        l_scr[...] = jnp.zeros(l_scr.shape, F32)
        lse_scr[...] = jnp.full(lse_scr.shape, NEG, F32)
        acc_t[...] = jnp.zeros(acc_t.shape, F32)

        def key_of(k):
            return jnp.maximum(g - k, 0)

        def score(h, blocks):
            return [dot(kv_all[key_of(k), 0], qt[:, cs(h)]) for k, _ in blocks]

        def keep_score(h, blocks, scores):
            mx = m_scr[:, cs(h)]
            for (k, keep), s in zip(blocks, scores):
                s = s * c_exp
                if keep is not None:
                    s = jnp.where(keep, s, NEG)
                s_scr[k, :, cs(h)] = s
                mx = jnp.maximum(mx, fold8(s, jnp.maximum))
            m_scr[:, cs(h)] = mx

        def softmax_pv(h, blocks, m_new):
            m_old = lse_scr[:, cs(h)]
            alpha = jnp.exp2(m_old - m_new)
            lse_scr[:, cs(h)] = m_new
            l_new = l_scr[:, cs(h)] * alpha
            pv = None
            for k, _ in blocks:
                p = jnp.exp2(s_scr[k, :, cs(h)] - m_new[0:1])
                l_new = l_new + fold8(p, jnp.add)
                part = dot(vt[key_of(k)], p.astype(BF16))
                pv = part if pv is None else pv + part
            l_scr[:, cs(h)] = l_new
            acc_t[:, cs(h)] = acc_t[:, cs(h)] * alpha[0:1] + pv

        def row_max(h):
            m = m_scr[:, cs(h)]
            return jnp.broadcast_to(jnp.max(m, axis=0, keepdims=True), m.shape)

        def fwd(new, old):
            if old:
                m_new = [row_max(h) for h in range(group)]
            for h in range(group):
                if new:
                    scores = score(h, new)
                if old:
                    softmax_pv(h, old, m_new[h])
                if new:
                    keep_score(h, new, scores)

        def pair(p):
            return [(2 * p, None), (2 * p + 1, None)]

        n_pair = n // 2
        odd = lax.rem(n, 2) == 1
        last = [(n - 1, diff > jnp.where(g >= n_win, 0, -2 * chunk))]
        fwd([(0, diff <= 0), (1, diff < jnp.where(g > 0, 2 * chunk, -2 * chunk))], None)

        def fwd_body(p, _):
            @pl.when((step == 0) & (p == need_1))
            def _():
                ready(top - 1)

            @pl.when((step == 0) & (p == need_2))
            def _():
                ready(top - 2)

            fwd(pair(p), pair(p - 1))
            return 0

        lax.fori_loop(1, n_pair, fwd_body, 0)

        @pl.when(odd)
        def _():
            @pl.when((step == 0) & (n_pair == need_2))
            def _():
                ready(top - 2)

            fwd(last, pair(n_pair - 1))
            fwd(None, last)

        @pl.when(jnp.logical_not(odd))
        def _():
            fwd(None, pair(n_pair - 1))

        l_row = jnp.sum(l_scr[...], axis=0, keepdims=True)
        lse_scr[...] = lse_scr[...] + jnp.log2(l_row)
        for h in range(group):
            o_t = (acc_t[:, cs(h)] / l_row[:, cs(h)]).astype(BF16)
            d = jnp.sum(o_t.astype(F32) * dot_t[:, cs(h)].astype(F32), axis=0, keepdims=True)
            d_scr[:, cs(h)] = jnp.broadcast_to(d, (8, chunk))
            o_st[i, h] = o_t.T
        acc_t[...] = jnp.zeros(acc_t.shape, F32)

        @pl.when(i != y)
        def _():
            out_copies(i)[0].start()

        @pl.when(step > 0)
        def _():
            reduce_start(i + 1)

        buf_a, buf_b = (p_a, s_a), (p_b, s_b)

        def grad(k1, buf1, k2, buf2):
            if k1 is not None:
                j1 = key_of(k1)
            if k2 is not None:
                j2 = key_of(k2)
                at = lax.rem(j2, 2) * half + j2 // 2
                pb, sb = buf2
            for h in range(group):
                if k1 is not None:
                    dp_t = dot(kv_all[j1, 1], dot_t[:, cs(h)])
                if k2 is not None:
                    if h == 0:
                        dkv[at, 1] += dot(pb[...], do_all[i].reshape(group * chunk, dim))
                    elif h == 1:
                        dkv[at, 0] += dot(sb[...], q_all[i].reshape(group * chunk, dim))
                    for e in range(group):
                        if min(2 + e // (group // 2), group - 1) == h:
                            acc_t[:, cs(e)] += dot(kt[j2], sb[:, cs(e)])
                if k1 is not None:
                    p = jnp.exp2(s_scr[k1, :, cs(h)] - lse_scr[0:1, cs(h)])
                    buf1[0][:, cs(h)] = p.astype(BF16)
                    buf1[1][:, cs(h)] = (p * (dp_t - d_scr[0:1, cs(h)])).astype(BF16)

        grad(0, buf_a, None, None)

        def bwd_body(t, _):
            grad(2 * t + 1, buf_b, 2 * t, buf_a)
            grad(2 * t + 2, buf_a, 2 * t + 1, buf_b)
            return 0

        lax.fori_loop(0, (n - 1) // 2, bwd_body, 0)

        @pl.when(odd)
        def _():
            grad(None, None, n - 1, buf_a)

        @pl.when(jnp.logical_not(odd))
        def _():
            grad(n - 1, buf_b, n - 2, buf_a)
            grad(None, None, n - 1, buf_b)

        for h in range(group):
            dq_st[i, h] = (acc_t[:, cs(h)] * sm_scale).astype(BF16).T

        @pl.when(i != y)
        def _():
            out_copies(i)[1].start()

        sib_copy(i).start()

        @pl.when(step == 0)
        def _():
            for s in slots[3:]:
                ready(s)
            for s in slots[1:]:
                wait_qdo(s)

        @pl.when(step > 0)
        def _():
            reduce_end(i + 1)

        return 0

    lax.fori_loop(0, n_y, one_chunk, 0)
    reduce_start(0)
    o_out[y] = o_st[y]
    dq_out[y] = dq_st[y]
    for d in yorder:
        for cp in [kv_copy(d)] + qdo_copies(d):
            cp.wait_send()
    for s in slots:
        sb_copy(s, 0).wait_send()
        for dx in xorder:
            ag_copy(s, dx).wait_send()
            sb_copy(s, dx).wait_send()
    reduce_end(0)
    dkv_out[y] = dkv_st[y]
    for yy in range(n_y):
        @pl.when(yy != y)
        def _():
            for k, out in enumerate((o_out, dq_out)):
                rcopy(o_st.at[yy], out.at[yy], od_s.at[k, yy], od_r.at[k, yy], sib).wait_recv()
            rcopy(dkv_st.at[yy], dkv_out.at[yy], fy_s.at[yy], fy_r.at[yy], sib).wait_recv()
            for cp in out_copies(yy):
                cp.wait_send()
            y_copy(yy).wait_send()

        sib_copy(yy).wait_send()
        for dx in xorder:
            x_copy(yy, dx).wait_send()


def solution(mesh):
    n_ctx = mesh.shape['ctx']
    seq_spec = P('dp', 'ctx', None, None)

    def local_attn(q_loc, k_loc, v_loc, do_loc):
        n_batch, chunk, q_heads, dim = q_loc.shape
        kv_heads = k_loc.shape[2]
        group = q_heads // kv_heads
        inner = n_ctx // kv_heads
        n_x = inner // 2
        n_win = WINDOW // chunk
        n_y = kv_heads
        wide = group * chunk

        def heads(x, per):
            return jnp.transpose(x[0], (1, 0, 2)).reshape(kv_heads, per, chunk, dim)

        def tokens(x):
            return jnp.transpose(x.reshape(-1, chunk, dim), (1, 0, 2))[None]

        q4, do4 = heads(q_loc, group), heads(do_loc, group)
        kv4 = jnp.concatenate([heads(k_loc, 1), heads(v_loc, 1)], axis=1)
        vm = pl.BlockSpec(memory_space=pltpu.VMEM)
        dma = pltpu.SemaphoreType.DMA
        o4, dq4, dkv4 = pl.pallas_call(
            functools.partial(attn_kernel, inner, n_win, dim ** -0.5),
            out_shape=(jax.ShapeDtypeStruct(q4.shape, BF16), jax.ShapeDtypeStruct(q4.shape, BF16),
                       jax.ShapeDtypeStruct(kv4.shape, BF16)),
            in_specs=[vm] * 3,
            out_specs=(vm,) * 3,
            scratch_shapes=[
                pltpu.VMEM(q4.shape, BF16), pltpu.VMEM(q4.shape, BF16), pltpu.VMEM((n_ctx, 2, chunk, dim), BF16),
                pltpu.VMEM((n_ctx, dim, chunk), BF16), pltpu.VMEM((n_ctx, dim, chunk), BF16),
                pltpu.VMEM((dim, wide), BF16), pltpu.VMEM((dim, wide), BF16),
                pltpu.VMEM((n_win + 1, chunk, wide), F32), pltpu.VMEM((dim, wide), F32),
                pltpu.VMEM((8, wide), F32), pltpu.VMEM((8, wide), F32),
                pltpu.VMEM((8, wide), F32), pltpu.VMEM((8, wide), F32),
                pltpu.VMEM((chunk, wide), BF16), pltpu.VMEM((chunk, wide), BF16),
                pltpu.VMEM((chunk, wide), BF16), pltpu.VMEM((chunk, wide), BF16),
                pltpu.VMEM((n_ctx, 2, chunk, dim), F32), pltpu.VMEM(q4.shape, BF16), pltpu.VMEM(q4.shape, BF16),
                pltpu.VMEM((n_ctx // 2, 2, chunk, dim), F32), pltpu.VMEM((n_x, n_y, 2, chunk, dim), F32),
                pltpu.VMEM(kv4.shape, BF16),
                dma((3,)), dma((3, n_y)), dma((3, n_y)), dma((n_y, n_x)), dma((n_y, n_x)), dma((n_y, n_x)), dma((n_y, n_x)),
                dma((2, n_y)), dma((2, n_y)), dma((n_y,)), dma((n_y,)), dma((n_y, n_x)), dma((n_y, n_x)),
                dma((n_y,)), dma((n_y,)),
            ],
            compiler_params=pltpu.CompilerParams(vmem_limit_bytes=63 * 1024 * 1024, collective_id=0, has_side_effects=True),
            name='attn_core',
        )(q4, do4, kv4)
        return tokens(o4), tokens(dq4), tokens(dkv4[:, 0]), tokens(dkv4[:, 1])

    return jax.shard_map(local_attn, mesh=mesh, in_specs=(seq_spec,) * 4, out_specs=(seq_spec,) * 4, check_vma=False)
```

time: 149 us -> 154 us (1.034); the launches traced: 147 us -> 154 us
  Pallas kernels: 135 us -> 142 us
    pallas_call x1, Pallas kernels: 135 us -> 142 us  [local_attn(): pl.pallas_call(functools.partial(attn_kernel, inner, n_win, dim ** (-0.5)...]
where the time goes in v5:
time: 154 us
  Pallas kernels  142 us (92%)
  local copies, waits for them, and re-layouts  10.2 us (7%)
    pallas_call x1, Pallas kernels, local_attn(): pl.pallas_call(functools.partial(attn_kernel, inner, n_win, dim ** (-0.5)...  142 us
    reshape x2, local copies, waits for them, and re-layouts, tokens(): return jnp.transpose(x.reshape(-1, chunk, dim), (1, 0, 2))[None]  4.61 us

profile of v5, /device:TPU:97, one launch (start us, length us, event | category | flops | bytes accessed | tf_op | source)
XLA Modules:
  0.0 154.1 jit_solution(2166878480492467712)
XLA Ops:
  0.6 0.0 copy-start
  0.6 1.2 copy_bitcast_fusion.2
  1.8 0.9 pad_maximum_fusion.kv_loc
  2.7 0.0 copy-done
  2.7 0.0 copy-start.1
  2.7 1.2 copy.8
  3.9 0.1 copy-done.1
  4.0 1.2 copy.9
  5.2 142.4 %attn_core.1 = (bf16[4,4,256,128]{3,2,1,0:T(8,128)(2,1)}, bf16[4,4,256,128]{3,2,1,0:T(8,128)(2,1)}, bf16[4,2,256,128]{3,2,1,0:T(8,128)(2,1)}) custom-call(bf16[4,4,256,128]{3,2,1,0:T(8,128)(2,1)} %bitcast.44, bf16[4,4,256,128]{3,2,1,0:T(8,128)(2,1)} %bitcast.45, bf16[4,2,256,128]{3,2,1,0:T(8,128)(2,1)} %pad_maximum_fusion.kv_loc), custom_call_target="tpu_custom_call" | custom-call | tf_op jit(solution)/shard_map/attn_core/pallas_call | solution.py:430
  147.7 0.0 copy-start.2
  147.7 3.0 %copy.21 = bf16[16,256,128]{2,0,1:T(8,128)(2,1)} copy(bf16[16,256,128]{2,1,0:T(8,128)(2,1)} %bitcast.51) | data formatting | bytes 2097152 | tf_op jit(solution)/shard_map/reshape | solution.py:424
  150.6 0.0 copy-done.2
  150.6 0.0 copy-start.3
  150.6 1.6 %copy.20 = bf16[16,256,128]{2,0,1:T(8,128)(2,1)} copy(bf16[16,256,128]{2,1,0:T(8,128)(2,1)S(1)} %bitcast.50) | data formatting | bytes 2097152 | tf_op jit(solution)/shard_map/reshape | solution.py:424
  152.3 0.0 copy-done.3
  152.3 0.9 copy.15
  153.2 0.9 copy.14
  (1 shorter events, 0.0 us)
Async XLA Ops:
  0.6 2.1 %copy-start = (bf16[1,256,16,128]{3,2,1,0:T(8,128)(2,1)S(1)}, bf16[1,256,16,128]{3,2,1,0:T(8,128)(2,1)}, u32[]{:S(2)}) copy-start(bf16[1,256,16,128]{3,2,1,0:T(8,128)(2,1)} %param.4) | copy-start | bytes 3145732
  2.7 1.3 copy-start.1
  147.7 3.0 %copy-start.2 = (bf16[4,4,256,128]{3,2,1,0:T(8,128)(2,1)S(1)}, bf16[4,4,256,128]{3,2,1,0:T(8,128)(2,1)}, u32[]{:S(2)}) copy-start(bf16[4,4,256,128]{3,2,1,0:T(8,128)(2,1)} %get-tuple-element.8) | copy-start | bytes 3145732
  150.6 1.7 %copy-start.3 = (bf16[4,2,256,128]{3,2,1,0:T(8,128)(2,1)S(1)}, bf16[4,2,256,128]{3,2,1,0:T(8,128)(2,1)}, u32[]{:S(2)}) copy-start(bf16[4,2,256,128]{3,2,1,0:T(8,128)(2,1)} %get-tuple-element.9) | copy-start | bytes 1572868

commit v6 on v5

--- a/solution.py
+++ b/solution.py
@@ -75,21 +75,24 @@
     def kv_copy(d):
         return rcopy(kv_loc.at[y_at(d)], kv_all.at[mine], in_s.at[0, d], in_r.at[0, d], dev(y_at(d), x, c))
 
-    def qdo_copies(d):
-        return [rcopy(src.at[y_at(d)], dst.at[y], in_s.at[k, d], in_r.at[k, d], dev(y_at(d), x, c))
-                for k, src, dst in ((1, q_loc, q_all), (2, do_loc, do_all))]
+    qdo = ((1, q_loc, q_all), (2, do_loc, do_all))
+
+    def qdo_copy(which, d):
+        k, src, dst = which
+        return rcopy(src.at[y_at(d)], dst.at[y], in_s.at[k, d], in_r.at[k, d], dev(y_at(d), x, c))
 
     def send_qdo():
-        for d in yorder:
-            for cp in qdo_copies(d):
-                cp.start()
-
-    def wait_qdo(s):
+        for which in qdo:
+            for d in yorder:
+                qdo_copy(which, d).start()
+
+    def wait_in(which, s):
+        k, _, dst = which
+
         @pl.when(s != y)
         def _():
             d = y_at(-s)
-            for k, dst in ((1, q_all), (2, do_all)):
-                rcopy(dst.at[s], dst.at[s], in_s.at[k, d], in_r.at[k, d], sib).wait_recv()
+            rcopy(dst.at[s], dst.at[s], in_s.at[k, d], in_r.at[k, d], sib).wait_recv()
 
     def ag_copy(s, dx):
         idx = s * inner + r
@@ -141,6 +144,10 @@
 
         lax.fori_loop(0, inner, prep, 0)
 
+    @pl.when(y != top)
+    def _():
+        send_qdo()
+
     ready(top)
 
     @pl.when(r == 0)
@@ -149,11 +156,7 @@
 
     locs[1].wait()
     locs[2].wait()
-    wait_qdo(top)
-
-    @pl.when(y != top)
-    def _():
-        send_qdo()
+    wait_in(qdo[0], top)
 
     need_1 = (r + 1) // 2
     need_2 = (r + inner + 1) // 2
@@ -206,7 +209,6 @@
         n = jnp.maximum(jnp.minimum(g, n_win) + 1, 2)
         for h in range(group):
             qt[:, cs(h)] = q_all[i, h].T
-            dot_t[:, cs(h)] = do_all[i, h].T
         m_scr[...] = jnp.full(m_scr.shape, NEG, F32)
         l_scr[...] = jnp.zeros(l_scr.shape, F32)
         lse_scr[...] = jnp.full(lse_scr.shape, NEG, F32)
@@ -292,6 +294,12 @@
         def _():
             fwd(None, pair(n_pair - 1))
 
+        @pl.when(step == 0)
+        def _():
+            wait_in(qdo[1], top)
+
+        for h in range(group):
+            dot_t[:, cs(h)] = do_all[i, h].T
         l_row = jnp.sum(l_scr[...], axis=0, keepdims=True)
         lse_scr[...] = lse_scr[...] + jnp.log2(l_row)
         for h in range(group):
@@ -304,10 +312,6 @@
         @pl.when(i != y)
         def _():
             out_copies(i)[0].start()
-
-        @pl.when(step > 0)
-        def _():
-            reduce_start(i + 1)
 
         buf_a, buf_b = (p_a, s_a), (p_b, s_b)
 
@@ -339,6 +343,11 @@
         def bwd_body(t, _):
             grad(2 * t + 1, buf_b, 2 * t, buf_a)
             grad(2 * t + 2, buf_a, 2 * t + 1, buf_b)
+
+            @pl.when((i > 0) & (t == r // 2))
+            def _():
+                sib_copy(i).start()
+
             return 0
 
         lax.fori_loop(0, (n - 1) // 2, bwd_body, 0)
@@ -359,14 +368,19 @@
         def _():
             out_copies(i)[1].start()
 
-        sib_copy(i).start()
+        @pl.when(i == 0)
+        def _():
+            sib_copy(i).start()
+
+        reduce_start(i)
 
         @pl.when(step == 0)
         def _():
             for s in slots[3:]:
                 ready(s)
             for s in slots[1:]:
-                wait_qdo(s)
+                for which in qdo:
+                    wait_in(which, s)
 
         @pl.when(step > 0)
         def _():
@@ -375,11 +389,10 @@
         return 0
 
     lax.fori_loop(0, n_y, one_chunk, 0)
-    reduce_start(0)
     o_out[y] = o_st[y]
     dq_out[y] = dq_st[y]
     for d in yorder:
-        for cp in [kv_copy(d)] + qdo_copies(d):
+        for cp in [kv_copy(d)] + [qdo_copy(which, d) for which in qdo]:
             cp.wait_send()
     for s in slots:
         sb_copy(s, 0).wait_send()

time: 154 us -> 130 us (0.84)
  Pallas kernels: 142 us -> 118 us
    pallas_call x1, Pallas kernels: 142 us -> 118 us  [local_attn(): pl.pallas_call(functools.partial(attn_kernel, inner, n_win, dim ** (-0.5)...]
where the time goes in v6:
time: 130 us; the launch traced here: 129 us
  Pallas kernels  118 us (91%)
  local copies, waits for them, and re-layouts  10.2 us (8%)
    pallas_call x1, Pallas kernels, local_attn(): pl.pallas_call(functools.partial(attn_kernel, inner, n_win, dim ** (-0.5)...  118 us
    reshape x2, local copies, waits for them, and re-layouts, tokens(): return jnp.transpose(x.reshape(-1, chunk, dim), (1, 0, 2))[None]  4.61 us

profile of v6, /device:TPU:97, one launch (start us, length us, event | category | flops | bytes accessed | tf_op | source)
XLA Modules:
  0.0 129.3 jit_solution(8531854047291931675)
XLA Ops:
  0.6 0.0 copy-start
  0.6 1.2 copy_bitcast_fusion.2
  1.8 0.9 pad_maximum_fusion.kv_loc
  2.7 0.0 copy-done
  2.7 0.0 copy-start.1
  2.7 1.2 copy.8
  3.9 0.1 copy-done.1
  4.0 1.2 copy.9
  5.2 117.6 %attn_core.1 = (bf16[4,4,256,128]{3,2,1,0:T(8,128)(2,1)}, bf16[4,4,256,128]{3,2,1,0:T(8,128)(2,1)}, bf16[4,2,256,128]{3,2,1,0:T(8,128)(2,1)}) custom-call(bf16[4,4,256,128]{3,2,1,0:T(8,128)(2,1)} %bitcast.44, bf16[4,4,256,128]{3,2,1,0:T(8,128)(2,1)} %bitcast.45, bf16[4,2,256,128]{3,2,1,0:T(8,128)(2,1)} %pad_maximum_fusion.kv_loc), custom_call_target="tpu_custom_call" | custom-call | tf_op jit(solution)/shard_map/attn_core/pallas_call | solution.py:443
  122.8 0.0 copy-start.2
  122.8 3.0 %copy.21 = bf16[16,256,128]{2,0,1:T(8,128)(2,1)} copy(bf16[16,256,128]{2,1,0:T(8,128)(2,1)} %bitcast.51) | data formatting | bytes 2097152 | tf_op jit(solution)/shard_map/reshape | solution.py:437
  125.8 0.0 copy-done.2
  125.8 0.0 copy-start.3
  125.8 1.6 %copy.20 = bf16[16,256,128]{2,0,1:T(8,128)(2,1)} copy(bf16[16,256,128]{2,1,0:T(8,128)(2,1)S(1)} %bitcast.50) | data formatting | bytes 2097152 | tf_op jit(solution)/shard_map/reshape | solution.py:437
  127.4 0.0 copy-done.3
  127.5 0.9 copy.15
  128.4 0.9 copy.14
  (1 shorter events, 0.0 us)
Async XLA Ops:
  0.6 2.1 %copy-start = (bf16[1,256,16,128]{3,2,1,0:T(8,128)(2,1)S(1)}, bf16[1,256,16,128]{3,2,1,0:T(8,128)(2,1)}, u32[]{:S(2)}) copy-start(bf16[1,256,16,128]{3,2,1,0:T(8,128)(2,1)} %param.4) | copy-start | bytes 3145732
  2.7 1.3 %copy-start.1 = (bf16[1,256,16,128]{3,2,1,0:T(8,128)(2,1)S(1)}, bf16[1,256,16,128]{3,2,1,0:T(8,128)(2,1)}, u32[]{:S(2)}) copy-start(bf16[1,256,16,128]{3,2,1,0:T(8,128)(2,1)} %param.7) | copy-start | bytes 3145732
  122.8 3.0 %copy-start.2 = (bf16[4,4,256,128]{3,2,1,0:T(8,128)(2,1)S(1)}, bf16[4,4,256,128]{3,2,1,0:T(8,128)(2,1)}, u32[]{:S(2)}) copy-start(bf16[4,4,256,128]{3,2,1,0:T(8,128)(2,1)} %get-tuple-element.8) | copy-start | bytes 3145732
  125.8 1.7 %copy-start.3 = (bf16[4,2,256,128]{3,2,1,0:T(8,128)(2,1)S(1)}, bf16[4,2,256,128]{3,2,1,0:T(8,128)(2,1)}, u32[]{:S(2)}) copy-start(bf16[4,2,256,128]{3,2,1,0:T(8,128)(2,1)} %get-tuple-element.9) | copy-start | bytes 1572868
